TPU v7x, 256 devices: a whole 4x4x8 slice. The times are simulated.
256 devices in a mesh: elem: 16 (over z, core), front: 16 (over y, x).
Axes of the slice: x: 4, y: 4, z: 8, core: 2. Of those that a mesh axis runs over, the one named last changes fastest.
Arguments:
- elem_mat: bfloat16 [24, 24, 32768], P(None, None, ('elem', 'front')), may hold values from -1.25 to 1.25
- elem_deriv: bfloat16 [24, 24, 32768], P(None, None, ('elem', 'front')), may hold values from -1.1953125 to 1.1953125
- elem_disp: bfloat16 [24, 32768], P(None, ('elem', 'front')), may hold values from -6 to 6
- elem_sens: bfloat16 [32768, 24, 512], P(('elem', 'front')), may hold values from -3 to 3
- design_var: int32 [32768], P(('elem', 'front')), may hold values from 0 to 511
- dof_rows: int32 [24, 32768], P(None, ('elem', 'front')), may hold values from 0 to 3584, as said below
- inverse_factor: bfloat16 [57344, 8192], P('front', 'elem'), may hold values from -2 to 2
- coupling: bfloat16 [8192, 49152], P('elem', 'front'), may hold values from -0.0625 to 0.0625
- front_sizes: int32 [7], replicated, may hold values from 4096 to 8192
Outputs:
- sens: float32 [57344, 512], P('front', 'elem')
Inputs may be any that keep to these rules, and one draw needn't show every extreme that they name: `dof_rows`: the used rows of one element lie in one aligned block of 128 rows; the value 3584 marks a degree of freedom that no front holds.
All inputs are finite; a program needn't handle non-finite values.
Results may differ from a plain program's by a relative error of at most 0.014.
Values may be sent and summed in bfloat16 or wider, within the bound.
No kernel may reach another device: no remote copies, remote signals or barrier semaphores. Data moves between devices by JAX's collectives and lax.ppermute only.
A program may use at most 128 MiB of HBM per device.

v0:
```python
import jax
import jax.numpy as jnp
from jax import lax
from jax.sharding import PartitionSpec as P

FS = 8192
LEVELS = 3


def swapped(array, axis, bit):
    return lax.ppermute(array, axis, [(i, i ^ 1 << bit) for i in range(lax.axis_size(axis))])


def form_loads(tables, derivs, disps, sens_block, variables, places, spot_rows):
    column_count = sens_block.shape[2]
    pseudo = -jnp.einsum("ije,ejc->eic", tables, sens_block, preferred_element_type=jnp.float32)
    drive_term = -jnp.einsum("ije,je->ei", derivs, disps, preferred_element_type=jnp.float32)
    column_ids = lax.iota(jnp.int32, column_count)
    hit_column = (column_ids[None, :] == variables[:, None]).astype(jnp.float32)
    pseudo = pseudo + drive_term[:, :, None] * hit_column[:, None, :]
    term_rows = jnp.zeros((spot_rows, column_count), jnp.float32)
    return term_rows.at[places.T.reshape(-1)].add(pseudo.reshape(-1, column_count), mode="drop")


def gather_group(local_block, bit_count, device):
    for bit_at in range(bit_count):
        partner = swapped(local_block, "front", bit_at)
        is_upper = device >> bit_at & 1 == 1
        local_block = jnp.where(
            is_upper,
            jnp.concatenate([partner, local_block], 0),
            jnp.concatenate([local_block, partner], 0),
        )
    return local_block


def reduce_group(partial_value, bit_count, device):
    for bit_at in reversed(range(bit_count)):
        half_rows = partial_value.shape[0] // 2
        lower_half = partial_value[:half_rows]
        upper_half = partial_value[half_rows:]
        is_upper = device >> bit_at & 1 == 1
        kept_half = jnp.where(is_upper, upper_half, lower_half)
        sent_half = jnp.where(is_upper, lower_half, upper_half)
        partial_value = kept_half + swapped(sent_half, "front", bit_at)
    return partial_value


def to_row_block(local_block, bit_count, device):
    whole_front = gather_group(local_block, bit_count, device)
    return lax.all_to_all(whole_front, "elem", split_axis=0, concat_axis=1, tiled=True)


def from_row_block(partial_value, bit_count, device):
    spread = lax.all_to_all(partial_value, "elem", split_axis=1, concat_axis=0, tiled=True)
    return reduce_group(spread, bit_count, device)


def body(
    elem_mat,
    elem_deriv,
    elem_disp,
    elem_sens,
    design_var,
    dof_rows,
    inverse_factor,
    coupling,
    front_sizes,
):
    front_count = lax.axis_size("front")
    depth_bits = front_count.bit_length() - 1
    device = lax.axis_index("front")
    spot_rows = inverse_factor.shape[0]
    term_rows = form_loads(
        elem_mat, elem_deriv, elem_disp, elem_sens, design_var, dof_rows, spot_rows
    )
    load_rows = lax.psum_scatter(term_rows, "elem", scatter_dimension=1, tiled=True)
    level_facts = []
    offset = 0
    first_front = 0
    for level_at in range(LEVELS):
        bit_count = depth_bits - (LEVELS - 1 - level_at)
        block_rows = FS >> bit_count
        front_id = first_front + (device >> bit_count)
        size_now = lax.dynamic_index_in_dim(front_sizes, front_id, 0, keepdims=False)
        rows_at = (device & (1 << bit_count) - 1) * block_rows + lax.iota(jnp.int32, block_rows)
        live_rows = (rows_at < size_now).astype(jnp.float32)[:, None]
        level_facts.append((bit_count, block_rows, offset, live_rows))
        offset = offset + block_rows
        first_front = first_front + (1 << LEVELS - 1 - level_at)
    forward_out = []
    acc_rows = None
    for level_at in range(LEVELS):
        bit_count, block_rows, offset, live_rows = level_facts[level_at]
        given = load_rows[offset : offset + block_rows]
        if acc_rows is not None:
            given = given - acc_rows
        rhs_in = (live_rows * given).astype(jnp.bfloat16)
        rhs_rows = to_row_block(rhs_in, bit_count, device)
        factor_rows = inverse_factor[offset : offset + block_rows]
        partial_value = jnp.dot(factor_rows, rhs_rows, preferred_element_type=jnp.float32)
        solved = live_rows * lax.psum_scatter(
            partial_value, "elem", scatter_dimension=1, tiled=True
        )
        forward_out.append(solved)
        if level_at < LEVELS - 1:
            wide_solved = lax.all_gather(solved.astype(jnp.bfloat16), "elem", axis=1, tiled=True)
            links = coupling[:, offset : offset + block_rows]
            parent_part = jnp.dot(links, wide_solved, preferred_element_type=jnp.float32)
            acc_rows = from_row_block(parent_part, bit_count + 1, device)
    pieces_out = [None] * LEVELS
    parent_rows = None
    for level_at in reversed(range(LEVELS)):
        bit_count, block_rows, offset, live_rows = level_facts[level_at]
        residual = forward_out[level_at]
        if parent_rows is not None:
            parent_block = to_row_block(parent_rows, bit_count + 1, device)
            links = coupling[:, offset : offset + block_rows]
            correction = lax.dot_general(
                links, parent_block, (((0,), (0,)), ((), ())), preferred_element_type=jnp.float32
            )
            residual = residual - lax.psum_scatter(
                correction, "elem", scatter_dimension=1, tiled=True
            )
        back_in = (live_rows * residual).astype(jnp.bfloat16)
        wide_back = lax.all_gather(back_in, "elem", axis=1, tiled=True)
        factor_rows = inverse_factor[offset : offset + block_rows]
        partial_value = lax.dot_general(
            factor_rows, wide_back, (((0,), (0,)), ((), ())), preferred_element_type=jnp.float32
        )
        answer = live_rows * from_row_block(partial_value, bit_count, device)
        pieces_out[level_at] = answer
        parent_rows = answer.astype(jnp.bfloat16)
    return jnp.concatenate(pieces_out, 0)


def solution(mesh):
    return jax.shard_map(
        body,
        mesh=mesh,
        in_specs=(
            P(None, None, ("elem", "front")),
            P(None, None, ("elem", "front")),
            P(None, ("elem", "front")),
            P(("elem", "front"), None, None),
            P(("elem", "front")),
            P(None, ("elem", "front")),
            P("front", "elem"),
            P("elem", "front"),
            P(),
        ),
        out_specs=P("front", "elem"),
        check_vma=False,
    )
```

profile of v0, /device:TPU:8, one launch (start us, length us, event | category | flops | bytes accessed | tf_op | source)
XLA Modules:
  0.0 1150.8 jit_solution(6993256583140113286)
XLA Ops:
  17.4 22.6 %scatter_custom_fusion = f32[3584,512]{1,0:T(8,128)} fusion(s32[3072]{0:T(1024)S(1)} %bitcast.153, f32[3072,512]{1,0:T(8,128)} %bitcast.117, f32[]{:T(128)} %constant.14.clone.1), kind=kCustom, calls=%fused_computation.2 | custom fusion | flops 1572864 | bytes 7340544 | tf_op jit(solution)/shard_map/scatter-add | solution.py:22
  40.0 8.4 copy.32
  50.4 70.2 %reduce-scatter.7.cloned.1.call-done = f32[3584,32]{0,1:T(8,128)} async-done(((f32[3584,512]{0,1:T(8,128)}), f32[3584,32]{0,1:T(8,128)}) %reduce-scatter.7.cloned.1.call-update) | async-done | bytes 458768 | tf_op jit(solution)/shard_map/reduce_scatter | solution.py:77
  135.3 19.5 %all_to_all.160 = bf16[16,512,32]{1,2,0:T(8,128)(2,1)S(1)} all-to-all(bf16[16,512,32]{1,2,0:T(8,128)(2,1)S(1)} %bitcast.137), channel_id=1, replica_groups=mesh['elem'=16,'front'=16] {'elem'}, dimensions={0} | all-to-all | bytes 1048576 | tf_op jit(solution)/shard_map/all_to_all | solution.py:51
  159.8 61.8 %reduce-scatter.9.cloned.1.call-done = f32[2048,32]{0,1:T(8,128)} async-done(((f32[2048,512]{0,1:T(8,128)}), f32[2048,32]{0,1:T(8,128)}) %reduce-scatter.9.cloned.1.call-update) | async-done | bytes 262160 | tf_op jit(solution)/shard_map/reduce_scatter | solution.py:102
  223.2 38.2 %all-gather.5.cloned.1.call-done = bf16[2048,512]{0,1:T(8,128)(2,1)} async-done(((bf16[2048,32]{0,1:T(8,128)(2,1)}), bf16[2048,512]{0,1:T(8,128)(2,1)}) %all-gather.5.cloned.1.call-update) | async-done | bytes 2097168 | tf_op jit(solution)/shard_map/all_gather | solution.py:107
  269.5 26.4 %all-to-all-done.1 = f32[512,16,32]{0,2,1:T(8,128)S(1)} async-done(((f32[512,16,32]{0,2,1:T(8,128)}), f32[512,16,32]{0,2,1:T(8,128)S(1)}, u32[]{:S(2)}, u32[]{:S(2)}) %all-to-all-start.1) | async-done | bytes 1048608 | tf_op jit(solution)/shard_map/all_to_all | solution.py:55
  296.8 13.3 %collective-permute-done.2 = f32[4096,32]{0,1:T(8,128)S(1)} collective-permute-done((f32[4096,32]{0,1:T(8,128)S(1)}, f32[4096,32]{0,1:T(8,128)S(1)}, u32[]{:S(2)}, u32[]{:S(2)}) %collective-permute-start.2) | collective-permute-done | bytes 524320 | tf_op jit(solution)/shard_map/ppermute | solution.py:11
  313.2 7.5 collective-permute-done.3
  345.1 18.9 %all_to_all.161 = bf16[16,512,32]{1,2,0:T(8,128)(2,1)S(1)} all-to-all(bf16[16,512,32]{1,2,0:T(8,128)(2,1)S(1)} %bitcast.138), channel_id=1, replica_groups=mesh['elem'=16,'front'=16] {'elem'}, dimensions={0} | all-to-all | bytes 1048576 | tf_op jit(solution)/shard_map/all_to_all | solution.py:51
  367.4 59.0 %reduce-scatter.11.cloned.1.call-done = f32[1024,32]{0,1:T(8,128)} async-done(((f32[1024,512]{0,1:T(8,128)}), f32[1024,32]{0,1:T(8,128)}) %reduce-scatter.11.cloned.1.call-update) | async-done | bytes 131088 | tf_op jit(solution)/shard_map/reduce_scatter | solution.py:102
  428.0 37.5 %all-gather.7.cloned.1.call-done = bf16[1024,512]{0,1:T(8,128)(2,1)} async-done(((bf16[1024,32]{0,1:T(8,128)(2,1)}), bf16[1024,512]{0,1:T(8,128)(2,1)}) %all-gather.7.cloned.1.call-update) | async-done | bytes 1048592 | tf_op jit(solution)/shard_map/all_gather | solution.py:107
  473.1 26.4 %all-to-all-done.3 = f32[512,16,32]{0,2,1:T(8,128)S(1)} async-done(((f32[512,16,32]{0,2,1:T(8,128)}), f32[512,16,32]{0,2,1:T(8,128)S(1)}, u32[]{:S(2)}, u32[]{:S(2)}) %all-to-all-start.3) | async-done | bytes 1048608 | tf_op jit(solution)/shard_map/all_to_all | solution.py:55
  501.9 13.2 %collective-permute-done.8 = f32[4096,32]{0,1:T(8,128)S(1)} collective-permute-done((f32[4096,32]{0,1:T(8,128)S(1)}, f32[4096,32]{0,1:T(8,128)S(1)}, u32[]{:S(2)}, u32[]{:S(2)}) %collective-permute-start.8) | collective-permute-done | bytes 524320 | tf_op jit(solution)/shard_map/ppermute | solution.py:11
  515.9 8.4 collective-permute-done.9
  560.7 19.7 %all_to_all.162 = bf16[16,512,32]{1,2,0:T(8,128)(2,1)S(1)} all-to-all(bf16[16,512,32]{1,2,0:T(8,128)(2,1)S(1)} %bitcast.139), channel_id=1, replica_groups=mesh['elem'=16,'front'=16] {'elem'}, dimensions={0} | all-to-all | bytes 1048576 | tf_op jit(solution)/shard_map/all_to_all | solution.py:51
  583.0 56.3 %reduce-scatter.13.cloned.1.call-done = f32[512,32]{0,1:T(8,128)} async-done(((f32[512,512]{0,1:T(8,128)}), f32[512,32]{0,1:T(8,128)}) %reduce-scatter.13.cloned.1.call-update) | async-done | bytes 65552 | tf_op jit(solution)/shard_map/reduce_scatter | solution.py:102
  640.1 15.7 %all_gather.17 = bf16[512,512]{0,1:T(8,128)(2,1)S(1)} all-gather(bf16[512,32]{0,1:T(8,128)(2,1)S(1)} %multiply_convert_fusion.4), channel_id=1, replica_groups=mesh['elem'=16,'front'=16] {'elem'}, dimensions={1}, use_global_device_ids=true | all-gather | bytes 557056 | tf_op jit(solution)/shard_map/all_gather | solution.py:126
  657.3 31.4 %all_to_all.163 = f32[512,16,32]{0,2,1:T(8,128)S(1)} all-to-all(f32[512,16,32]{0,2,1:T(8,128)S(1)} %bitcast.123), channel_id=1, replica_groups=mesh['elem'=16,'front'=16] {'elem'}, dimensions={1} | all-to-all | bytes 2097152 | tf_op jit(solution)/shard_map/all_to_all | solution.py:55
  691.2 13.4 %collective-permute-done.16 = f32[4096,32]{0,1:T(8,128)S(1)} collective-permute-done((f32[4096,32]{0,1:T(8,128)S(1)}, f32[4096,32]{0,1:T(8,128)S(1)}, u32[]{:S(2)}, u32[]{:S(2)}) %collective-permute-start.16) | collective-permute-done | bytes 524320 | tf_op jit(solution)/shard_map/ppermute | solution.py:11
  705.5 8.0 collective-permute-done.17
  713.6 12.2 %collective-permute-start.18 = (f32[1024,32]{0,1:T(8,128)S(1)}, f32[1024,32]{0,1:T(8,128)S(1)}, u32[]{:S(2)}, u32[]{:S(2)}) collective-permute-start(f32[1024,32]{0,1:T(8,128)S(1)} %slice_select_fusion.6), channel_id=1, source_target_pairs={{0,2},{1,3},{2,0},{3,1},{4,6},{5,7},{6,4},{7,5},{8,10},{9,11},{10,... | collective-permute-start | bytes 393224 | tf_op jit(solution)/shard_map/ppermute | solution.py:11
  758.0 19.2 %all_to_all.164 = bf16[16,512,32]{1,2,0:T(8,128)(2,1)S(1)} all-to-all(bf16[16,512,32]{1,2,0:T(8,128)(2,1)S(1)} %bitcast.140), channel_id=1, replica_groups=mesh['elem'=16,'front'=16] {'elem'}, dimensions={0} | all-to-all | bytes 1048576 | tf_op jit(solution)/shard_map/all_to_all | solution.py:51
  780.6 58.9 %reduce-scatter.15.cloned.1.call-done = f32[1024,32]{0,1:T(8,128)} async-done(((f32[1024,512]{0,1:T(8,128)}), f32[1024,32]{0,1:T(8,128)}) %reduce-scatter.15.cloned.1.call-update) | async-done | bytes 131088 | tf_op jit(solution)/shard_map/reduce_scatter | solution.py:122
  841.1 37.1 %all-gather.9.cloned.1.call-done = bf16[1024,512]{0,1:T(8,128)(2,1)} async-done(((bf16[1024,32]{0,1:T(8,128)(2,1)}), bf16[1024,512]{0,1:T(8,128)(2,1)}) %all-gather.9.cloned.1.call-update) | async-done | bytes 1048592 | tf_op jit(solution)/shard_map/all_gather | solution.py:126
  880.5 31.3 %all_to_all.165 = f32[512,16,32]{0,2,1:T(8,128)S(1)} all-to-all(f32[512,16,32]{0,2,1:T(8,128)S(1)} %bitcast.145), channel_id=1, replica_groups=mesh['elem'=16,'front'=16] {'elem'}, dimensions={1} | all-to-all | bytes 2097152 | tf_op jit(solution)/shard_map/all_to_all | solution.py:55
  912.7 13.5 %collective-permute-done.24 = f32[4096,32]{0,1:T(8,128)S(1)} collective-permute-done((f32[4096,32]{0,1:T(8,128)S(1)}, f32[4096,32]{0,1:T(8,128)S(1)}, u32[]{:S(2)}, u32[]{:S(2)}) %collective-permute-start.24) | collective-permute-done | bytes 524320 | tf_op jit(solution)/shard_map/ppermute | solution.py:11
  959.5 18.5 %all_to_all.166 = bf16[16,512,32]{1,2,0:T(8,128)(2,1)S(1)} all-to-all(bf16[16,512,32]{1,2,0:T(8,128)(2,1)S(1)} %bitcast.141), channel_id=1, replica_groups=mesh['elem'=16,'front'=16] {'elem'}, dimensions={0} | all-to-all | bytes 1048576 | tf_op jit(solution)/shard_map/all_to_all | solution.py:51
  981.5 62.5 %reduce-scatter.17.cloned.1.call-done = f32[2048,32]{0,1:T(8,128)} async-done(((f32[2048,512]{0,1:T(8,128)}), f32[2048,32]{0,1:T(8,128)}) %reduce-scatter.17.cloned.1.call-update) | async-done | bytes 262160 | tf_op jit(solution)/shard_map/reduce_scatter | solution.py:122
  1045.6 37.9 %all-gather.11.cloned.1.call-done = bf16[2048,512]{0,1:T(8,128)(2,1)} async-done(((bf16[2048,32]{0,1:T(8,128)(2,1)}), bf16[2048,512]{0,1:T(8,128)(2,1)}) %all-gather.11.cloned.1.call-update) | async-done | bytes 2097168 | tf_op jit(solution)/shard_map/all_gather | solution.py:126
  1087.0 31.2 %all_to_all.167 = f32[512,16,32]{0,2,1:T(8,128)S(1)} all-to-all(f32[512,16,32]{0,2,1:T(8,128)S(1)} %bitcast.146), channel_id=1, replica_groups=mesh['elem'=16,'front'=16] {'elem'}, dimensions={1} | all-to-all | bytes 2097152 | tf_op jit(solution)/shard_map/all_to_all | solution.py:55
  1121.5 12.6 %collective-permute-done.30 = f32[4096,32]{0,1:T(8,128)S(1)} collective-permute-done((f32[4096,32]{0,1:T(8,128)S(1)}, f32[4096,32]{0,1:T(8,128)S(1)}, u32[]{:S(2)}, u32[]{:S(2)}) %collective-permute-start.30) | collective-permute-done | bytes 524320 | tf_op jit(solution)/shard_map/ppermute | solution.py:11
  (185 shorter events, 225.6 us)
Async XLA Ops:
  6.5 114.0 %reduce-scatter.7.cloned.1.call-start = ((), (), s32[]{:S(2)}) async-start(), calls=%async_computation.16 | async-start | bytes 7798784 | tf_op jit(solution)/shard_map/reduce_scatter | solution.py:77
  48.5 173.1 %reduce-scatter.9.cloned.1.call-start = ((), (), s32[]{:S(2)}) async-start(), calls=%async_computation.17 | async-start | bytes 4456448 | tf_op jit(solution)/shard_map/reduce_scatter | solution.py:102
  126.8 8.3 collective-permute-start.1
  159.7 101.7 %all-gather.5.cloned.1.call-start = ((), (), s32[]{:S(2)}) async-start(), calls=%async_computation.18 | async-start | bytes 2228224 | tf_op jit(solution)/shard_map/all_gather | solution.py:107
  265.3 30.7 %all-to-all-start.1 = ((f32[512,16,32]{0,2,1:T(8,128)}), f32[512,16,32]{0,2,1:T(8,128)S(1)}, u32[]{:S(2)}, u32[]{:S(2)}) async-start(f32[512,16,32]{0,2,1:T(8,128)} %bitcast.144), calls=%async_computation.3 | async-start | bytes 2097152 | tf_op jit(solution)/shard_map/all_to_all | solution.py:55
  269.5 156.9 %reduce-scatter.11.cloned.1.call-start = ((), (), s32[]{:S(2)}) async-start(), calls=%async_computation.19 | async-start | bytes 2228224 | tf_op jit(solution)/shard_map/reduce_scatter | solution.py:102
  296.1 13.9 %collective-permute-start.2 = (f32[4096,32]{0,1:T(8,128)S(1)}, f32[4096,32]{0,1:T(8,128)S(1)}, u32[]{:S(2)}, u32[]{:S(2)}) collective-permute-start(f32[4096,32]{0,1:T(8,128)S(1)} %bitcast.147), channel_id=1, source_target_pairs={{0,4},{1,5},{2,6},{3,7},{4,0},{5,1},{6,2},{7,3},{8,12},{9,13},{10,... | collective-permute-start | bytes 1572872 | tf_op jit(solution)/shard_map/ppermute | solution.py:11
  310.2 10.6 collective-permute-start.3
  331.8 6.6 collective-permute-start.6
  338.4 6.5 collective-permute-start.7
  367.3 98.1 %all-gather.7.cloned.1.call-start = ((), (), s32[]{:S(2)}) async-start(), calls=%async_computation.20 | async-start | bytes 1114112 | tf_op jit(solution)/shard_map/all_gather | solution.py:107
  468.7 30.9 %all-to-all-start.3 = ((f32[512,16,32]{0,2,1:T(8,128)}), f32[512,16,32]{0,2,1:T(8,128)S(1)}, u32[]{:S(2)}, u32[]{:S(2)}) async-start(f32[512,16,32]{0,2,1:T(8,128)} %bitcast.18), calls=%async_computation.6 | async-start | bytes 2097152 | tf_op jit(solution)/shard_map/all_to_all | solution.py:55
  473.0 166.2 %reduce-scatter.13.cloned.1.call-start = ((), (), s32[]{:S(2)}) async-start(), calls=%async_computation.21 | async-start | bytes 1114112 | tf_op jit(solution)/shard_map/reduce_scatter | solution.py:102
  499.7 15.4 %collective-permute-start.8 = (f32[4096,32]{0,1:T(8,128)S(1)}, f32[4096,32]{0,1:T(8,128)S(1)}, u32[]{:S(2)}, u32[]{:S(2)}) collective-permute-start(f32[4096,32]{0,1:T(8,128)S(1)} %bitcast.148), channel_id=1, source_target_pairs={{0,8},{1,9},{2,10},{3,11},{4,12},{5,13},{6,14},{7,15},{8,0},{9,1},... | collective-permute-start | bytes 1572872 | tf_op jit(solution)/shard_map/ppermute | solution.py:11
  515.2 9.1 collective-permute-start.9
  524.4 6.9 collective-permute-start.10
  552.5 8.0 collective-permute-start.15
  583.0 256.5 %reduce-scatter.15.cloned.1.call-start = ((), (), s32[]{:S(2)}) async-start(), calls=%async_computation.22 | async-start | bytes 2228224 | tf_op jit(solution)/shard_map/reduce_scatter | solution.py:122
  688.9 15.7 %collective-permute-start.16 = (f32[4096,32]{0,1:T(8,128)S(1)}, f32[4096,32]{0,1:T(8,128)S(1)}, u32[]{:S(2)}, u32[]{:S(2)}) collective-permute-start(f32[4096,32]{0,1:T(8,128)S(1)} %bitcast.149), channel_id=1, source_target_pairs={{0,8},{1,9},{2,10},{3,11},{4,12},{5,13},{6,14},{7,15},{8,0},{9,1},... | collective-permute-start | bytes 1572872 | tf_op jit(solution)/shard_map/ppermute | solution.py:11
  704.7 8.8 collective-permute-start.17
  713.6 15.6 %collective-permute-start.18 = (f32[1024,32]{0,1:T(8,128)S(1)}, f32[1024,32]{0,1:T(8,128)S(1)}, u32[]{:S(2)}, u32[]{:S(2)}) collective-permute-start(f32[1024,32]{0,1:T(8,128)S(1)} %slice_select_fusion.6), channel_id=1, source_target_pairs={{0,2},{1,3},{2,0},{3,1},{4,6},{5,7},{6,4},{7,5},{8,10},{9,11},{10,... | collective-permute-start | bytes 393224 | tf_op jit(solution)/shard_map/ppermute | solution.py:11
  743.6 6.2 collective-permute-start.22
  749.9 8.0 collective-permute-start.23
  780.5 97.7 %all-gather.9.cloned.1.call-start = ((), (), s32[]{:S(2)}) async-start(), calls=%async_computation.23 | async-start | bytes 1114112 | tf_op jit(solution)/shard_map/all_gather | solution.py:126
  841.1 202.9 %reduce-scatter.17.cloned.1.call-start = ((), (), s32[]{:S(2)}) async-start(), calls=%async_computation.24 | async-start | bytes 4456448 | tf_op jit(solution)/shard_map/reduce_scatter | solution.py:122
  912.0 14.2 %collective-permute-start.24 = (f32[4096,32]{0,1:T(8,128)S(1)}, f32[4096,32]{0,1:T(8,128)S(1)}, u32[]{:S(2)}, u32[]{:S(2)}) collective-permute-start(f32[4096,32]{0,1:T(8,128)S(1)} %bitcast.150), channel_id=1, source_target_pairs={{0,4},{1,5},{2,6},{3,7},{4,0},{5,1},{6,2},{7,3},{8,12},{9,13},{10,... | collective-permute-start | bytes 1572872 | tf_op jit(solution)/shard_map/ppermute | solution.py:11
  926.3 10.3 collective-permute-start.25
  946.3 6.6 collective-permute-start.28
  952.9 6.5 collective-permute-start.29
  981.4 102.1 %all-gather.11.cloned.1.call-start = ((), (), s32[]{:S(2)}) async-start(), calls=%async_computation.25 | async-start | bytes 2228224 | tf_op jit(solution)/shard_map/all_gather | solution.py:126
  1118.4 15.7 %collective-permute-start.30 = (f32[4096,32]{0,1:T(8,128)S(1)}, f32[4096,32]{0,1:T(8,128)S(1)}, u32[]{:S(2)}, u32[]{:S(2)}) collective-permute-start(f32[4096,32]{0,1:T(8,128)S(1)} %bitcast.151), channel_id=1, source_target_pairs={{0,2},{1,3},{2,0},{3,1},{4,6},{5,7},{6,4},{7,5},{8,10},{9,11},{10,... | collective-permute-start | bytes 1572872 | tf_op jit(solution)/shard_map/ppermute | solution.py:11
  1134.1 8.8 collective-permute-start.31
  (19 other events, 388.8 us)
Sparse Core Ops, SparseCore 0:
  48.6 71.9 reduce-scatter.6
  159.9 61.6 reduce-scatter.8
  223.4 37.9 all-gather.4
  367.5 58.8 reduce-scatter.10
  428.1 37.2 all-gather.6
  583.1 56.1 reduce-scatter.12
  780.6 58.8 reduce-scatter.14
  841.3 36.8 all-gather.8
  981.5 62.3 reduce-scatter.16
  1045.7 37.7 all-gather.10
where the time goes:
time: 1160 us; the launch traced here: 1150 us
  waiting for transfers between devices  761 us (66%)
  blocking collectives  206 us (18%)
  starting transfers between devices  80.1 us (7%)
  other arithmetic  40.2 us (3%)
  matrix products  36.6 us (3%)
  between operations  14.2 us (1%)
  local copies, waits for them, and re-layouts  13.6 us (1%)
    ppermute x32, waiting for transfers between devices, swapped(): lax.ppermute(array, axis, [(i, i ^ 1 << bit) for i in range(lax.axis_size...  188 us
    reduce_scatter x3, waiting for transfers between devices, body(): lax.psum_scatter(partial_value, 'elem', scatter_dimension=1, tiled=True)  177 us
    reduce_scatter x2, waiting for transfers between devices, body(): lax.psum_scatter(correction, 'elem', scatter_dimension=1, tiled=True)  121 us
    all_to_all x5, blocking collectives, to_row_block(): lax.all_to_all(whole_front, 'elem', split_axis=0, concat_axis=1, tiled=True)  95.9 us
    all_to_all x3, blocking collectives, from_row_block(): lax.all_to_all(partial_value, 'elem', split_axis=1, concat_axis=0, tiled=...  93.9 us
    all_gather x2, waiting for transfers between devices, body(): lax.all_gather(solved.astype(jnp.bfloat16), 'elem', axis=1, tiled=True)  75.6 us
    all_gather x2, waiting for transfers between devices, body(): wide_back = lax.all_gather(back_in, 'elem', axis=1, tiled=True)  75.1 us
    ppermute x32, starting transfers between devices, swapped(): lax.ppermute(array, axis, [(i, i ^ 1 << bit) for i in range(lax.axis_size...  71.2 us
  transfers between devices with their start and end apart: 44, of which 44 were waited for; matrix products, arithmetic and copies ran while one was open for 0% of the time, Pallas kernels for 0%

commit v1 on v0

v1 whole, which is shorter than its diff:
```python
import jax
import jax.numpy as jnp
from jax import lax
from jax.sharding import Mesh
from jax.sharding import PartitionSpec as P

FS = 8192
LR = 3584
NRHS = 512
BF = jnp.bfloat16
F32 = jnp.float32

Z, C, H, L, X = "z", "c", "h", "l", "x"
FRONT = (H, L, X)
PAIR = (L, X)


def dot_t(a, b):
    return lax.dot_general(a, b, (((1,), (1,)), ((), ())), preferred_element_type=F32)


def dot(a, b):
    return lax.dot_general(a, b, (((1,), (0,)), ((), ())), preferred_element_type=F32)


def exchange(chunks, axes):
    return lax.all_to_all(chunks, axes, split_axis=0, concat_axis=0, tiled=True)


def reduce_chunks(chunks, axes):
    return jnp.sum(exchange(chunks.astype(BF), axes).astype(F32), axis=0)


def gather_chunks(chunk, axes, count):
    return exchange(jnp.broadcast_to(chunk[None], (count,) + chunk.shape), axes)


def form_loads(tables, derivs, disps, sens_block, variables, places):
    pseudo = -jnp.einsum("ije,ejc->eic", tables, sens_block, preferred_element_type=F32)
    drive_term = -jnp.einsum("ije,je->ei", derivs, disps, preferred_element_type=F32)
    column_ids = lax.iota(jnp.int32, NRHS)
    hit_column = (column_ids[None, :] == variables[:, None]).astype(F32)
    pseudo = pseudo + drive_term[:, :, None] * hit_column[:, None, :]
    term_rows = jnp.zeros((LR, NRHS), F32)
    return term_rows.at[places.T.reshape(-1)].add(pseudo.reshape(-1, NRHS), mode="drop")


def pair_up(is_first, own, other, axis):
    first = jnp.where(is_first, own, other)
    second = jnp.where(is_first, other, own)
    return jnp.concatenate([first, second], axis)


def body(
    elem_mat,
    elem_deriv,
    elem_disp,
    elem_sens,
    design_var,
    dof_rows,
    inverse_factor,
    coupling,
    front_sizes,
):
    z = lax.axis_index(Z)
    c = lax.axis_index(C)
    h = lax.axis_index(H)
    l = lax.axis_index(L)
    x = lax.axis_index(X)
    core_swap = [(0, 1), (1, 0)]
    is_c0 = c == 0

    w0 = lax.all_gather(inverse_factor[0:2048], (C, X), axis=0, tiled=False).reshape(2, FS, 512)
    g0 = lax.all_gather(coupling[:, 0:2048], (C, X), axis=0, tiled=False).reshape(2, 4, 512, 2048)
    w2 = lax.all_gather(inverse_factor[3072:3584], (C, H, L, X), axis=0, tiled=False).reshape(2, FS, 512)
    w1_own = inverse_factor[2048:3072]
    g1_own = coupling[:, 2048:3072]
    w1_other = lax.ppermute(w1_own, C, core_swap)
    g1_other = lax.ppermute(g1_own, C, core_swap)

    block_rows = z * 1024 + lax.iota(jnp.int32, 1024)

    def mask_of(front, rows):
        size = lax.dynamic_index_in_dim(front_sizes, front, 0, keepdims=False)
        return (rows < size).astype(F32)[None, :]

    mask0 = mask_of(h * 2 + l, block_rows)
    mask1 = mask_of(4 + h, block_rows)
    mask1f = mask_of(4 + h, (l * 4 + x) * 1024 + lax.iota(jnp.int32, 1024))
    mask2 = mask_of(6, block_rows)

    term_rows = form_loads(elem_mat, elem_deriv, elem_disp, elem_sens, design_var, dof_rows)
    term_cols = term_rows.astype(BF).T.reshape(8, 2, 32, LR)
    halves = exchange(term_cols.transpose(1, 0, 2, 3), C).astype(F32)
    half = halves[0] + halves[1]
    top = half[:, :, :2048].astype(BF).reshape(2, 4, 32, 2048).transpose(1, 0, 2, 3)
    top = exchange(top, X)
    top = top.reshape(4, 2, 32, 2, 1024).transpose(0, 3, 1, 2, 4).reshape(8, 64, 1024)
    load0 = reduce_chunks(top, Z)

    rest = lax.psum_scatter(half[:, :, 2048:], Z, scatter_dimension=0, tiled=True)[0]
    turn = [(zz * 8 + ss, ss * 8 + zz) for zz in range(8) for ss in range(8)]
    load1 = lax.ppermute(rest[:, :1024], (Z, L, X), turn)
    rest2 = rest[:, 1024:].reshape(2, 16, 512)
    is_even = (x & 1) == 0
    got = []
    for k in range(2):
        sent = jnp.where(is_even, rest2[k], rest2[1 - k])
        perm = [
            (zz * 16 + ff, (ff >> 1) * 16 + ((ff & 1) ^ k) * 8 + zz)
            for zz in range(8)
            for ff in range(16)
        ]
        got.append(lax.ppermute(sent, (Z, H, L, X), perm))
    load2 = pair_up(h == 0, got[0], got[1], 1)

    rhs0 = (mask0 * load0).astype(BF)
    y0_part = dot_t(rhs0[:, :512], w0[0]) + dot_t(rhs0[:, 512:], w0[1])
    y0 = mask0 * reduce_chunks(y0_part.reshape(64, 8, 1024).transpose(1, 0, 2), Z)
    y0_all = gather_chunks(y0.astype(BF), Z, 8).transpose(1, 0, 2).reshape(64, FS)
    acc0 = []
    for at in range(2):
        acc0.append(
            sum(dot_t(y0_all[:, s * 2048 : s * 2048 + 2048], g0[at, s]) for s in range(4))
        )
    acc0 = jnp.concatenate(acc0, 1).reshape(2, 32, 1024)
    is_l0 = l == 0
    acc0_kept = jnp.where(is_l0, acc0[0], acc0[1])
    acc0_sent = jnp.where(is_l0, acc0[1], acc0[0])
    acc0_sum = acc0_kept + lax.ppermute(acc0_sent, L, core_swap)

    rhs1 = (mask1 * (load1 - acc0_sum)).astype(BF)
    rhs1 = gather_chunks(rhs1, PAIR, 8).reshape(256, 1024)

    def by_core(value):
        return (
            jnp.where(is_c0, value[:, :512], value[:, 512:]),
            jnp.where(is_c0, value[:, 512:], value[:, :512]),
        )

    rhs1_own, rhs1_other = by_core(rhs1)
    y1_part = dot_t(rhs1_own, w1_own) + dot_t(rhs1_other, w1_other)
    y1 = mask1f * reduce_chunks(y1_part.reshape(8, 32, 1024), Z)
    y1_all = gather_chunks(y1.astype(BF), Z, 8).reshape(256, 1024)
    acc1 = pair_up(is_c0, dot_t(y1_all, g1_own).astype(BF), dot_t(y1_all, g1_other).astype(BF), 1)
    acc1 = acc1.reshape(8, 2, 16, 1024).transpose(1, 0, 2, 3).reshape(16, 16, 1024)
    acc1_sum = reduce_chunks(acc1, FRONT)

    rhs2 = (mask2 * (load2 - acc1_sum)).astype(BF)
    y2_part = dot_t(rhs2[:, :512], w2[0]) + dot_t(rhs2[:, 512:], w2[1])
    y2 = mask2 * reduce_chunks(y2_part.reshape(16, 8, 1024).transpose(1, 0, 2), Z)
    back2 = gather_chunks(y2.astype(BF), Z, 8).transpose(1, 0, 2).reshape(16, FS)
    x2 = mask2 * jnp.concatenate([dot(back2, w2[0]), dot(back2, w2[1])], 1)
    got = []
    for k in range(2):
        sent = jnp.where((h ^ k) == 0, x2[:, :512], x2[:, 512:])
        perm = [
            (zz * 16 + ff, (ff & 7) * 16 + 2 * zz + ((ff >> 3) ^ k))
            for zz in range(8)
            for ff in range(16)
        ]
        got.append(lax.ppermute(sent, (Z, H, L, X), perm))
    out2 = pair_up(is_even, got[0], got[1], 0)
    x2_all = gather_chunks(x2.astype(BF), FRONT, 16)
    x2_all = x2_all.reshape(2, 8, 16, 1024).transpose(1, 0, 2, 3).reshape(256, 1024)

    x2_own, x2_other = by_core(x2_all)
    corr1 = dot(x2_own, g1_own) + dot(x2_other, g1_other)
    z1 = y1 - reduce_chunks(corr1.reshape(8, 32, 1024), Z)
    back1 = gather_chunks((mask1f * z1).astype(BF), Z, 8).reshape(256, 1024)
    x1_part = pair_up(is_c0, dot(back1, w1_own).astype(BF), dot(back1, w1_other).astype(BF), 1)
    x1 = mask1 * reduce_chunks(x1_part.reshape(8, 32, 1024), PAIR)
    out1 = lax.ppermute(x1, (Z, L, X), turn)
    x1_round = x1.astype(BF)
    x1_pair = pair_up(is_l0, x1_round, lax.ppermute(x1_round, L, core_swap), 0)

    corr0 = []
    for s in range(4):
        corr0.append(dot(x1_pair[:, :512], g0[0, s]) + dot(x1_pair[:, 512:], g0[1, s]))
    corr0 = jnp.stack(corr0, 0).reshape(4, 64, 2, 1024).transpose(0, 2, 1, 3).reshape(8, 64, 1024)
    z0 = y0 - reduce_chunks(corr0, Z)
    back0 = gather_chunks((mask0 * z0).astype(BF), Z, 8).transpose(1, 0, 2).reshape(64, FS)
    x0 = mask0 * jnp.concatenate([dot(back0, w0[0]), dot(back0, w0[1])], 1)
    x0 = x0.reshape(2, 32, 1024)
    got = []
    for k in range(2):
        sent = jnp.where(((z & 1) ^ k) == 0, x0[0], x0[1])
        perm = [
            (zz * 4 + xx, (xx + 4 * ((zz & 1) ^ k)) * 4 + (zz >> 1))
            for zz in range(8)
            for xx in range(4)
        ]
        got.append(lax.ppermute(sent, (Z, X), perm))
    out0 = pair_up(z < 4, got[0], got[1], 1)
    return jnp.concatenate([out0, out1, out2], 1).T


def solution(mesh):
    fine = Mesh(mesh.devices.reshape(8, 2, 2, 2, 4), (Z, C, H, L, X))
    elem, front = (Z, C), (H, L, X)
    both = elem + front
    return jax.shard_map(
        body,
        mesh=fine,
        in_specs=(
            P(None, None, both),
            P(None, None, both),
            P(None, both),
            P(both, None, None),
            P(both),
            P(None, both),
            P(front, elem),
            P(elem, front),
            P(),
        ),
        out_specs=P(front, elem),
        check_vma=False,
    )
```

time: 1160 us -> 564 us (0.49)
  waiting for transfers between devices: 761 us -> 119 us
  matrix products: 36.6 us -> 78.1 us
  blocking collectives: 206 us -> 181 us
  local copies, waits for them, and re-layouts: 13.6 us -> 33.8 us
    reduce_scatter x6 -> x1, waiting for transfers between devices: 369 us -> 0.03 us  [body(): lax.psum_scatter(half[:, :, 2048:], Z, scatter_dimension=0, tiled=True)[0]]
    ppermute x32 -> x12, waiting for transfers between devices: 188 us -> 19.9 us  [the longest x1 9.14 us: body(): out1 = lax.ppermute(x1, (Z, L, X), turn)]
    all_gather x4 -> x3, waiting for transfers between devices: 151 us -> 0.04 us  [the longest x1 0.02 us: body(): lax.all_gather(inverse_factor[0:2048], (C, X), axis=0, tiled=False)]
    all_to_all x2 -> x7, waiting for transfers between devices: 52.9 us -> 98.5 us  [exchange(): return lax.all_to_all(chunks, axes, split_axis=0, concat_axis=0, tiled=True)]
    dot_general x11 -> x33, matrix products: 36.6 us -> 78.1 us  [the longest x16 51.4 us: dot_t(): lax.dot_general(a, b, (((1,), (1,)), ((), ())), preferred_element_type=F32)]
    all_to_all x2 -> x7, starting transfers between devices: 8.55 us -> 43.3 us  [exchange(): return lax.all_to_all(chunks, axes, split_axis=0, concat_axis=0, tiled=True)]
    ppermute x32 -> x12, starting transfers between devices: 71.2 us -> 41.3 us  [the longest x4 16.9 us: body(): got.append(lax.ppermute(sent, (Z, H, L, X), perm))]
    all_gather x1 -> x0, blocking collectives: 15.7 us -> none  [body(): wide_back = lax.all_gather(back_in, 'elem', axis=1, tiled=True)]
  transfers between devices with their start and end apart: 44 -> 23, of which waited for: 44 -> 12; matrix products, arithmetic and copies ran while one was open for 0% -> 22% of each run, Pallas kernels for 0% -> 0%
where the time goes in v1:
time: 564 us; the launch traced here: 555 us
  blocking collectives  181 us (32%)
  waiting for transfers between devices  119 us (21%)
  starting transfers between devices  84.8 us (15%)
  matrix products  78.1 us (14%)
  other arithmetic  42.8 us (8%)
  local copies, waits for them, and re-layouts  33.8 us (6%)
  between operations  15.9 us (3%)
    all_to_all x10, blocking collectives, exchange(): return lax.all_to_all(chunks, axes, split_axis=0, concat_axis=0, tiled=True)  181 us
    all_to_all x7, waiting for transfers between devices, exchange(): return lax.all_to_all(chunks, axes, split_axis=0, concat_axis=0, tiled=True)  98.5 us
    dot_general x16, matrix products, dot_t(): lax.dot_general(a, b, (((1,), (1,)), ((), ())), preferred_element_type=F32)  51.4 us
    all_to_all x7, starting transfers between devices, exchange(): return lax.all_to_all(chunks, axes, split_axis=0, concat_axis=0, tiled=True)  43.3 us
    scatter-add x1, other arithmetic, form_loads(): term_rows.at[places.T.reshape(-1)]  22.5 us
    dot_general x16, matrix products, dot(): lax.dot_general(a, b, (((1,), (0,)), ((), ())), preferred_element_type=F32)  21.7 us
    ppermute x4, starting transfers between devices, body(): got.append(lax.ppermute(sent, (Z, H, L, X), perm))  16.9 us
  transfers between devices with their start and end apart: 23, of which 12 were waited for; matrix products, arithmetic and copies ran while one was open for 22% of the time, Pallas kernels for 0%

profile of v1, /device:TPU:8, one launch (start us, length us, event | category | flops | bytes accessed | tf_op | source)
XLA Modules:
  0.0 554.8 jit_solution(9286456391678944227)
XLA Ops:
  17.6 22.5 %scatter_custom_fusion = f32[3584,512]{1,0:T(8,128)} fusion(s32[3072]{0:T(1024)S(1)} %bitcast.199, f32[3072,512]{1,0:T(8,128)} %bitcast.162, f32[]{:T(128)} %constant.50.clone.1), kind=kCustom, calls=%fused_computation.24 | custom fusion | flops 1572864 | bytes 7340544 | tf_op jit(solution)/shard_map/scatter-add | solution.py:45
  40.1 5.5 convert_bitcast_fusion
  45.6 6.1 %copy.27 = bf16[512,3584]{1,0:T(8,128)(2,1)} copy(bf16[512,3584]{0,1:T(8,128)(2,1)} %convert_bitcast_fusion) | data formatting | bytes 7340032 | tf_op jit(solution)/shard_map/transpose | solution.py:93
  54.0 7.0 %all_to_all.85 = bf16[2,8,32,3584]{3,2,1,0:T(8,128)(2,1)S(1)} all-to-all(bf16[2,8,32,3584]{3,2,1,0:T(8,128)(2,1)S(1)} %bitcast.161), channel_id=1, replica_groups=mesh['z'=8,'c'=2,'h'=2,'l'=2,'x'=4] {'c'}, dimensions={0} | all-to-all | bytes 7340032 | tf_op jit(solution)/shard_map/all_to_all | solution.py:27
  71.0 32.0 %all_to_all.86 = bf16[4,2,32,2048]{3,2,1,0:T(8,128)(2,1)S(1)} all-to-all(bf16[4,2,32,2048]{3,2,1,0:T(8,128)(2,1)S(1)} %bitcast.167), channel_id=1, replica_groups=mesh['z'=8,'c'=2,'h'=2,'l'=2,'x'=4] {'x'}, dimensions={0} | all-to-all | bytes 2097152 | tf_op jit(solution)/shard_map/all_to_all | solution.py:27
  105.1 8.4 %all-to-all-start.2 = ((bf16[8,64,1024]{2,1,0:T(8,128)(2,1)}), bf16[8,64,1024]{2,1,0:T(8,128)(2,1)S(1)}, u32[]{:S(2)}, u32[]{:S(2)}) async-start(bf16[8,64,1024]{2,1,0:T(8,128)(2,1)} %bitcast.13), calls=%async_computation.2 | async-start | bytes 2097152 | tf_op jit(solution)/shard_map/all_to_all | solution.py:27
  114.9 26.6 %all-to-all-done.2 = bf16[8,64,1024]{2,1,0:T(8,128)(2,1)S(1)} async-done(((bf16[8,64,1024]{2,1,0:T(8,128)(2,1)}), bf16[8,64,1024]{2,1,0:T(8,128)(2,1)S(1)}, u32[]{:S(2)}, u32[]{:S(2)}) %all-to-all-start.2) | async-done | bytes 1048608 | tf_op jit(solution)/shard_map/all_to_all | solution.py:27
  141.7 6.0 %fusion.12 = f32[64,8192]{1,0:T(8,128)S(1)} fusion(bf16[16384,512]{1,0:T(8,128)(2,1)} %all-gather.7.cloned.1.call-done, bf16[64,1024]{1,0:T(8,128)(2,1)S(1)} %multiply_convert_fusion.1), kind=kOutput, calls=%fused_computation.15 | convolution fusion | flops 536870912 | bytes 10551296 | tf_op jit(solution)/shard_map/dot_general | solution.py:19
  147.7 6.0 %fusion = bf16[64,8192]{1,0:T(8,128)(2,1)S(1)} fusion(f32[64,8192]{1,0:T(8,128)S(1)} %fusion.12, bf16[16384,512]{1,0:T(8,128)(2,1)} %all-gather.7.cloned.1.call-done, bf16[64,1024]{1,0:T(8,128)(2,1)S(1)} %multiply_convert_fusion.1), kind=kOutput, calls=%fused_computation.2 | convolution fusion | flops 537919488 | bytes 11599872 | tf_op jit(solution)/shard_map/dot_general | solution.py:19
  153.8 31.9 %all_to_all.87 = bf16[8,64,1024]{2,1,0:T(8,128)(2,1)S(1)} all-to-all(bf16[8,64,1024]{2,1,0:T(8,128)(2,1)S(1)} %bitcast.169), channel_id=1, replica_groups=mesh['z'=8,'c'=2,'h'=2,'l'=2,'x'=4] {'z'}, dimensions={0} | all-to-all | bytes 2097152 | tf_op jit(solution)/shard_map/all_to_all | solution.py:27
  191.6 7.6 %collective-permute-start = (f32[32,1024]{1,0:T(8,128)S(1)}, f32[32,1024]{1,0:T(8,128)}, u32[]{:S(2)}, u32[]{:S(2)}) collective-permute-start(f32[32,1024]{1,0:T(8,128)S(1)} %slice.247), channel_id=1, source_target_pairs={{0,0},{1,32},{2,64},{3,96},{4,128},{5,160},{6,192},{7,224},{32,1},... | collective-permute-start | bytes 393224 | tf_op jit(solution)/shard_map/ppermute | solution.py:103
  199.2 18.6 %all-to-all-done.4 = bf16[8,64,1024]{2,1,0:T(8,128)(2,1)S(1)} async-done(((bf16[8,64,1024]{2,1,0:T(8,128)(2,1)}), bf16[8,64,1024]{2,1,0:T(8,128)(2,1)S(1)}, u32[]{:S(2)}, u32[]{:S(2)}) %all-to-all-start.4) | async-done | bytes 1048608 | tf_op jit(solution)/shard_map/all_to_all | solution.py:27
  245.0 9.0 %all-to-all-start.5 = ((bf16[8,32,1024]{2,1,0:T(8,128)(2,1)}), bf16[8,32,1024]{2,1,0:T(8,128)(2,1)}, u32[]{:S(2)}, u32[]{:S(2)}) async-start(bf16[8,32,1024]{2,1,0:T(8,128)(2,1)} %broadcast_in_dim.18), calls=%async_computation.6 | async-start | bytes 1048576 | tf_op jit(solution)/shard_map/all_to_all | solution.py:27
  254.0 11.9 %all-to-all-done.5 = bf16[8,32,1024]{2,1,0:T(8,128)(2,1)} async-done(((bf16[8,32,1024]{2,1,0:T(8,128)(2,1)}), bf16[8,32,1024]{2,1,0:T(8,128)(2,1)}, u32[]{:S(2)}, u32[]{:S(2)}) %all-to-all-start.5) | async-done | bytes 524320 | tf_op jit(solution)/shard_map/all_to_all | solution.py:27
  270.6 6.0 %all-to-all-start.6 = ((bf16[8,32,1024]{2,1,0:T(8,128)(2,1)}), bf16[8,32,1024]{2,1,0:T(8,128)(2,1)}, u32[]{:S(2)}, u32[]{:S(2)}) async-start(bf16[8,32,1024]{2,1,0:T(8,128)(2,1)} %bitcast.177), calls=%async_computation.7 | async-start | bytes 1048576 | tf_op jit(solution)/shard_map/all_to_all | solution.py:27
  277.2 16.8 %all-to-all-done.6 = bf16[8,32,1024]{2,1,0:T(8,128)(2,1)} async-done(((bf16[8,32,1024]{2,1,0:T(8,128)(2,1)}), bf16[8,32,1024]{2,1,0:T(8,128)(2,1)}, u32[]{:S(2)}, u32[]{:S(2)}) %all-to-all-start.6) | async-done | bytes 524320 | tf_op jit(solution)/shard_map/all_to_all | solution.py:27
  301.2 16.8 %all-to-all-done.7 = bf16[8,32,1024]{2,1,0:T(8,128)(2,1)} async-done(((bf16[8,32,1024]{2,1,0:T(8,128)(2,1)}), bf16[8,32,1024]{2,1,0:T(8,128)(2,1)}, u32[]{:S(2)}, u32[]{:S(2)}) %all-to-all-start.7) | async-done | bytes 524320 | tf_op jit(solution)/shard_map/all_to_all | solution.py:27
  322.4 8.7 %all-to-all-start.8 = ((bf16[16,16,1024]{2,1,0:T(8,128)(2,1)}), bf16[16,16,1024]{2,1,0:T(8,128)(2,1)}, u32[]{:S(2)}, u32[]{:S(2)}) async-start(bf16[16,16,1024]{2,1,0:T(8,128)(2,1)} %bitcast.173), calls=%async_computation.9 | async-start | bytes 1048576 | tf_op jit(solution)/shard_map/all_to_all | solution.py:27
  350.2 5.8 %fusion.5 = f32[16,8192]{1,0:T(8,128)S(1)} fusion(bf16[16384,512]{1,0:T(8,128)(2,1)} %all-gather.11.cloned.1.call-done, bf16[16,1024]{1,0:T(8,128)(2,1)} %fusion.75), kind=kOutput, calls=%fused_computation.8 | convolution fusion | flops 134217728 | bytes 8929280 | tf_op jit(solution)/shard_map/dot_general | solution.py:19
  356.0 6.4 %fusion.1 = bf16[16,8192]{1,0:T(8,128)(2,1)S(1)} fusion(f32[16,8192]{1,0:T(8,128)S(1)} %fusion.5, bf16[16384,512]{1,0:T(8,128)(2,1)} %all-gather.11.cloned.1.call-done, bf16[16,1024]{1,0:T(8,128)(2,1)} %fusion.75), kind=kOutput, calls=%fused_computation.4 | convolution fusion | flops 134479872 | bytes 9191424 | tf_op jit(solution)/shard_map/dot_general | solution.py:19
  362.5 15.2 %all_to_all.88 = bf16[8,16,1024]{2,1,0:T(8,128)(2,1)S(1)} all-to-all(bf16[8,16,1024]{2,1,0:T(8,128)(2,1)S(1)} %bitcast.192), channel_id=1, replica_groups=mesh['z'=8,'c'=2,'h'=2,'l'=2,'x'=4] {'z'}, dimensions={0} | all-to-all | bytes 524288 | tf_op jit(solution)/shard_map/all_to_all | solution.py:27
  377.7 12.9 %all_to_all.89 = bf16[8,16,1024]{2,1,0:T(8,128)(2,1)S(1)} all-to-all(bf16[8,16,1024]{2,1,0:T(8,128)(2,1)S(1)} %broadcast_in_dim.20), channel_id=1, replica_groups=mesh['z'=8,'c'=2,'h'=2,'l'=2,'x'=4] {'z'}, dimensions={0} | all-to-all | bytes 524288 | tf_op jit(solution)/shard_map/all_to_all | solution.py:27
  393.8 16.1 %all_to_all.90 = bf16[16,16,1024]{2,1,0:T(8,128)(2,1)S(1)} all-to-all(bf16[16,16,1024]{2,1,0:T(8,128)(2,1)S(1)} %broadcast_in_dim.21), channel_id=1, replica_groups=mesh['z'=8,'c'=2,'h'=2,'l'=2,'x'=4] {'h','l','x'}, dimensions={0} | all-to-all | bytes 1048576 | tf_op jit(solution)/shard_map/all_to_all | solution.py:27
  412.0 15.7 %all_to_all.91 = bf16[8,32,1024]{2,1,0:T(8,128)(2,1)S(1)} all-to-all(bf16[8,32,1024]{2,1,0:T(8,128)(2,1)S(1)} %bitcast.178), channel_id=1, replica_groups=mesh['z'=8,'c'=2,'h'=2,'l'=2,'x'=4] {'z'}, dimensions={0} | all-to-all | bytes 1048576 | tf_op jit(solution)/shard_map/all_to_all | solution.py:27
  427.9 16.0 %all_to_all.92 = bf16[8,32,1024]{2,1,0:T(8,128)(2,1)S(1)} all-to-all(bf16[8,32,1024]{2,1,0:T(8,128)(2,1)S(1)} %broadcast_in_dim.22), channel_id=1, replica_groups=mesh['z'=8,'c'=2,'h'=2,'l'=2,'x'=4] {'z'}, dimensions={0} | all-to-all | bytes 1048576 | tf_op jit(solution)/shard_map/all_to_all | solution.py:27
  447.2 11.9 %all_to_all.93 = bf16[8,32,1024]{2,1,0:T(8,128)(2,1)S(1)} all-to-all(bf16[8,32,1024]{2,1,0:T(8,128)(2,1)S(1)} %bitcast.175), channel_id=1, replica_groups=mesh['z'=8,'c'=2,'h'=2,'l'=2,'x'=4] {'l','x'}, dimensions={0} | all-to-all | bytes 1048576 | tf_op jit(solution)/shard_map/all_to_all | solution.py:27
  468.4 22.2 %all_to_all.94 = bf16[8,64,1024]{2,1,0:T(8,128)(2,1)S(1)} all-to-all(bf16[8,64,1024]{2,1,0:T(8,128)(2,1)S(1)} %bitcast.165), channel_id=1, replica_groups=mesh['z'=8,'c'=2,'h'=2,'l'=2,'x'=4] {'z'}, dimensions={0} | all-to-all | bytes 2097152 | tf_op jit(solution)/shard_map/all_to_all | solution.py:27
  495.6 7.8 %collective-permute-start.10 = (f32[16,512]{1,0:T(8,128)S(1)}, f32[16,512]{1,0:T(8,128)S(1)}, u32[]{:S(2)}, u32[]{:S(2)}) collective-permute-start(f32[16,512]{1,0:T(8,128)S(1)} %get-tuple-element.27), channel_id=1, source_target_pairs={{0,0},{1,32},{2,64},{3,96},{4,128},{5,160},{6,192},{7,224},{8,1},{... | collective-permute-start | bytes 98312 | tf_op jit(solution)/shard_map/ppermute | solution.py:162
  506.1 7.8 %all-to-all-done.16 = bf16[8,64,1024]{2,1,0:T(8,128)(2,1)S(1)} async-done(((bf16[8,64,1024]{2,1,0:T(8,128)(2,1)}), bf16[8,64,1024]{2,1,0:T(8,128)(2,1)S(1)}, u32[]{:S(2)}, u32[]{:S(2)}) %all-to-all-start.16) | async-done | bytes 1048608 | tf_op jit(solution)/shard_map/all_to_all | solution.py:27
  514.0 5.1 fusion.14
  524.8 9.9 %collective-permute-start.8 = (f32[32,1024]{1,0:T(8,128)S(1)}, f32[32,1024]{1,0:T(8,128)S(1)}, u32[]{:S(2)}, u32[]{:S(2)}) collective-permute-start(f32[32,1024]{1,0:T(8,128)S(1)} %get-tuple-element.18), channel_id=1, source_target_pairs={{0,128},{1,160},{2,192},{3,224},{32,0},{33,32},{34,64},{35,96},{64... | collective-permute-start | bytes 393224 | tf_op jit(solution)/shard_map/ppermute | solution.py:193
  537.3 9.1 %collective-permute-done.9 = f32[32,1024]{1,0:T(8,128)S(1)} collective-permute-done((f32[32,1024]{1,0:T(8,128)S(1)}, f32[32,1024]{1,0:T(8,128)S(1)}, u32[]{:S(2)}, u32[]{:S(2)}) %collective-permute-start.9) | collective-permute-done | bytes 131104 | tf_op jit(solution)/shard_map/ppermute | solution.py:173
  (177 shorter events, 129.5 us)
Async XLA Ops:
  7.4 134.3 %all-gather.7.cloned.1.call-start = ((), (), s32[]{:S(2)}) async-start(), calls=%async_computation.19 | async-start | bytes 18874368 | tf_op jit(solution)/shard_map/all_gather | solution.py:73
  10.6 180.0 %reduce-scatter.2.cloned.1.call-start = ((), (), s32[]{:S(2)}) async-start(), calls=%async_computation.18 | async-start | bytes 1769472 | tf_op jit(solution)/shard_map/reduce_scatter | solution.py:101
  65.6 152.3 %all-gather.9.cloned.1.call-start = ((), (), s32[]{:S(2)}) async-start(), calls=%async_computation.20 | async-start | bytes 18874368 | tf_op jit(solution)/shard_map/all_gather | solution.py:74
  67.2 283.0 %all-gather.11.cloned.1.call-start = ((), (), s32[]{:S(2)}) async-start(), calls=%async_computation.21 | async-start | bytes 17301504 | tf_op jit(solution)/shard_map/all_gather | solution.py:75
  69.1 44.4 %copy-start.12 = (s32[7]{0:T(128)S(1)}, s32[7]{0:T(128)}, u32[]{:S(2)}) copy-start(s32[7]{0:T(128)} %param.17) | copy-start | bytes 88
  105.1 36.4 %all-to-all-start.2 = ((bf16[8,64,1024]{2,1,0:T(8,128)(2,1)}), bf16[8,64,1024]{2,1,0:T(8,128)(2,1)S(1)}, u32[]{:S(2)}, u32[]{:S(2)}) async-start(bf16[8,64,1024]{2,1,0:T(8,128)(2,1)} %bitcast.13), calls=%async_computation.2 | async-start | bytes 2097152 | tf_op jit(solution)/shard_map/all_to_all | solution.py:27
  187.1 30.7 %all-to-all-start.4 = ((bf16[8,64,1024]{2,1,0:T(8,128)(2,1)}), bf16[8,64,1024]{2,1,0:T(8,128)(2,1)S(1)}, u32[]{:S(2)}, u32[]{:S(2)}) async-start(bf16[8,64,1024]{2,1,0:T(8,128)(2,1)} %broadcast_in_dim.17), calls=%async_computation.5 | async-start | bytes 2097152 | tf_op jit(solution)/shard_map/all_to_all | solution.py:27
  191.6 51.0 %collective-permute-start = (f32[32,1024]{1,0:T(8,128)S(1)}, f32[32,1024]{1,0:T(8,128)}, u32[]{:S(2)}, u32[]{:S(2)}) collective-permute-start(f32[32,1024]{1,0:T(8,128)S(1)} %slice.247), channel_id=1, source_target_pairs={{0,0},{1,32},{2,64},{3,96},{4,128},{5,160},{6,192},{7,224},{32,1},... | collective-permute-start | bytes 393224 | tf_op jit(solution)/shard_map/ppermute | solution.py:103
  236.9 63.3 %copy-start.5 = (bf16[512,3072]{1,0:T(8,128)(2,1)S(1)}, bf16[512,3072]{1,0:T(8,128)(2,1)}, u32[]{:S(2)}) copy-start(bf16[512,3072]{1,0:T(8,128)(2,1)} %param.16) | copy-start | bytes 9437188
  236.9 6.3 %collective-permute-start.1 = (f32[32,1024]{1,0:T(8,128)S(1)}, f32[32,1024]{1,0:T(8,128)S(1)}, u32[]{:S(2)}, u32[]{:S(2)}) collective-permute-start(f32[32,1024]{1,0:T(8,128)S(1)} %broadcast_select_fusion.6), channel_id=1, source_target_pairs={{0,4},{4,0},{1,5},{5,1},{2,6},{6,2},{3,7},{7,3},{8,12},{12,8},{9,1... | collective-permute-start | bytes 393224 | tf_op jit(solution)/shard_map/ppermute | solution.py:130
  242.0 25.8 %collective-permute-start.2 = (bf16[1024,512]{1,0:T(8,128)(2,1)}, bf16[1024,512]{1,0:T(8,128)(2,1)}, u32[]{:S(2)}, u32[]{:S(2)}) collective-permute-start(bf16[1024,512]{1,0:T(8,128)(2,1)} %slice.216), channel_id=1, source_target_pairs={{0,16},{16,0},{1,17},{17,1},{2,18},{18,2},{3,19},{19,3},{4,20},{20... | collective-permute-start | bytes 3145736 | tf_op jit(solution)/shard_map/ppermute | solution.py:78
  245.0 20.9 %all-to-all-start.5 = ((bf16[8,32,1024]{2,1,0:T(8,128)(2,1)}), bf16[8,32,1024]{2,1,0:T(8,128)(2,1)}, u32[]{:S(2)}, u32[]{:S(2)}) async-start(bf16[8,32,1024]{2,1,0:T(8,128)(2,1)} %broadcast_in_dim.18), calls=%async_computation.6 | async-start | bytes 1048576 | tf_op jit(solution)/shard_map/all_to_all | solution.py:27
  270.6 23.4 %all-to-all-start.6 = ((bf16[8,32,1024]{2,1,0:T(8,128)(2,1)}), bf16[8,32,1024]{2,1,0:T(8,128)(2,1)}, u32[]{:S(2)}, u32[]{:S(2)}) async-start(bf16[8,32,1024]{2,1,0:T(8,128)(2,1)} %bitcast.177), calls=%async_computation.7 | async-start | bytes 1048576 | tf_op jit(solution)/shard_map/all_to_all | solution.py:27
  296.0 22.0 %all-to-all-start.7 = ((bf16[8,32,1024]{2,1,0:T(8,128)(2,1)}), bf16[8,32,1024]{2,1,0:T(8,128)(2,1)}, u32[]{:S(2)}, u32[]{:S(2)}) async-start(bf16[8,32,1024]{2,1,0:T(8,128)(2,1)} %broadcast_in_dim.19), calls=%async_computation.8 | async-start | bytes 1048576 | tf_op jit(solution)/shard_map/all_to_all | solution.py:27
  301.2 18.3 %collective-permute-start.5 = (bf16[512,1024]{1,0:T(8,128)(2,1)}, bf16[512,1024]{1,0:T(8,128)(2,1)}, u32[]{:S(2)}, u32[]{:S(2)}) collective-permute-start(bf16[512,1024]{1,0:T(8,128)(2,1)} %slice.219), channel_id=1, source_target_pairs={{0,16},{16,0},{1,17},{17,1},{2,18},{18,2},{3,19},{19,3},{4,20},{20... | collective-permute-start | bytes 3145736 | tf_op jit(solution)/shard_map/ppermute | solution.py:79
  322.4 25.3 %all-to-all-start.8 = ((bf16[16,16,1024]{2,1,0:T(8,128)(2,1)}), bf16[16,16,1024]{2,1,0:T(8,128)(2,1)}, u32[]{:S(2)}, u32[]{:S(2)}) async-start(bf16[16,16,1024]{2,1,0:T(8,128)(2,1)} %bitcast.173), calls=%async_computation.9 | async-start | bytes 1048576 | tf_op jit(solution)/shard_map/all_to_all | solution.py:27
  332.5 11.2 %collective-permute-start.3 = (f32[16,512]{1,0:T(8,128)}, f32[16,512]{1,0:T(8,128)}, u32[]{:S(2)}, u32[]{:S(2)}) collective-permute-start(f32[16,512]{1,0:T(8,128)} %get-tuple-element.19), channel_id=1, source_target_pairs={{0,0},{1,8},{2,32},{3,40},{4,64},{5,72},{6,96},{7,104},{8,128},{9,... | collective-permute-start | bytes 98312 | tf_op jit(solution)/shard_map/ppermute | solution.py:114
  334.4 11.9 %collective-permute-start.4 = (f32[16,512]{1,0:T(8,128)}, f32[16,512]{1,0:T(8,128)}, u32[]{:S(2)}, u32[]{:S(2)}) collective-permute-start(f32[16,512]{1,0:T(8,128)} %get-tuple-element.20), channel_id=1, source_target_pairs={{0,8},{1,0},{2,40},{3,32},{4,72},{5,64},{6,104},{7,96},{8,136},{9,... | collective-permute-start | bytes 98312 | tf_op jit(solution)/shard_map/ppermute | solution.py:114
  350.2 40.5 %copy-start.2 = (bf16[16384,512]{1,0:T(8,128)(2,1)S(1)}, bf16[16384,512]{1,0:T(8,128)(2,1)}, u32[]{:S(2)}) copy-start(bf16[16384,512]{1,0:T(8,128)(2,1)} %all-gather.11.cloned.1.call-done) | copy-start | bytes 50331652
  390.7 73.5 %slice-start = ((s8[16777216]{0:T(1024)(128)(4,1)}), s8[4194304]{0:T(1024)(128)(4,1)S(1)}, s32[]{:S(2)}) async-start(s8[16777216]{0:T(1024)(128)(4,1)} %bitcast.150), calls=%async_computation.22 | async-start | bytes 8388608
  391.9 72.3 %slice-start.1 = ((s8[16777216]{0:T(1024)(128)(4,1)}), s8[4194304]{0:T(1024)(128)(4,1)S(1)}, s32[]{:S(2)}) async-start(s8[16777216]{0:T(1024)(128)(4,1)} %bitcast.150), calls=%async_computation.23 | async-start | bytes 8388608
  393.8 70.4 %slice-start.2 = ((s8[16777216]{0:T(1024)(128)(4,1)}), s8[4194304]{0:T(1024)(128)(4,1)S(1)}, s32[]{:S(2)}) async-start(s8[16777216]{0:T(1024)(128)(4,1)} %bitcast.150), calls=%async_computation.24 | async-start | bytes 8388608
  427.9 36.3 %slice-start.3 = ((s8[16777216]{0:T(1024)(128)(4,1)}), s8[4194304]{0:T(1024)(128)(4,1)S(1)}, s32[]{:S(2)}) async-start(s8[16777216]{0:T(1024)(128)(4,1)} %bitcast.150), calls=%async_computation.25 | async-start | bytes 8388608
  459.8 4.3 collective-permute-start.6
  468.2 27.3 %copy-start.6 = (f32[16,1024]{1,0:T(8,128)S(1)}, f32[16,1024]{1,0:T(8,128)}, u32[]{:S(2)}) copy-start(f32[16,1024]{1,0:T(8,128)} %get-tuple-element.8) | copy-start | bytes 196612
  492.0 21.9 %all-to-all-start.16 = ((bf16[8,64,1024]{2,1,0:T(8,128)(2,1)}), bf16[8,64,1024]{2,1,0:T(8,128)(2,1)S(1)}, u32[]{:S(2)}, u32[]{:S(2)}) async-start(bf16[8,64,1024]{2,1,0:T(8,128)(2,1)} %broadcast_in_dim.23), calls=%async_computation.17 | async-start | bytes 2097152 | tf_op jit(solution)/shard_map/all_to_all | solution.py:27
  495.6 39.1 %collective-permute-start.10 = (f32[16,512]{1,0:T(8,128)S(1)}, f32[16,512]{1,0:T(8,128)S(1)}, u32[]{:S(2)}, u32[]{:S(2)}) collective-permute-start(f32[16,512]{1,0:T(8,128)S(1)} %get-tuple-element.27), channel_id=1, source_target_pairs={{0,0},{1,32},{2,64},{3,96},{4,128},{5,160},{6,192},{7,224},{8,1},{... | collective-permute-start | bytes 98312 | tf_op jit(solution)/shard_map/ppermute | solution.py:162
  503.4 31.3 %collective-permute-start.11 = (f32[16,512]{1,0:T(8,128)S(1)}, f32[16,512]{1,0:T(8,128)S(1)}, u32[]{:S(2)}, u32[]{:S(2)}) collective-permute-start(f32[16,512]{1,0:T(8,128)S(1)} %get-tuple-element.28), channel_id=1, source_target_pairs={{0,1},{1,33},{2,65},{3,97},{4,129},{5,161},{6,193},{7,225},{8,0},{... | collective-permute-start | bytes 98312 | tf_op jit(solution)/shard_map/ppermute | solution.py:162
  514.0 33.2 %copy-start.1 = (bf16[128,24,512]{2,1,0:T(8,128)(2,1)S(1)}, bf16[128,24,512]{2,1,0:T(8,128)(2,1)}, u32[]{:S(2)}) copy-start(bf16[128,24,512]{2,1,0:T(8,128)(2,1)} %param.12) | copy-start | bytes 9437188
  524.1 12.5 %collective-permute-start.7 = (f32[32,1024]{1,0:T(8,128)S(1)}, f32[32,1024]{1,0:T(8,128)S(1)}, u32[]{:S(2)}, u32[]{:S(2)}) collective-permute-start(f32[32,1024]{1,0:T(8,128)S(1)} %get-tuple-element.17), channel_id=1, source_target_pairs={{0,0},{1,32},{2,64},{3,96},{32,128},{33,160},{34,192},{35,224},{64... | collective-permute-start | bytes 393224 | tf_op jit(solution)/shard_map/ppermute | solution.py:193
  524.8 12.4 %collective-permute-start.8 = (f32[32,1024]{1,0:T(8,128)S(1)}, f32[32,1024]{1,0:T(8,128)S(1)}, u32[]{:S(2)}, u32[]{:S(2)}) collective-permute-start(f32[32,1024]{1,0:T(8,128)S(1)} %get-tuple-element.18), channel_id=1, source_target_pairs={{0,128},{1,160},{2,192},{3,224},{32,0},{33,32},{34,64},{35,96},{64... | collective-permute-start | bytes 393224 | tf_op jit(solution)/shard_map/ppermute | solution.py:193
  534.7 11.7 %collective-permute-start.9 = (f32[32,1024]{1,0:T(8,128)S(1)}, f32[32,1024]{1,0:T(8,128)S(1)}, u32[]{:S(2)}, u32[]{:S(2)}) collective-permute-start(f32[32,1024]{1,0:T(8,128)S(1)} %copy-done.9), channel_id=1, source_target_pairs={{0,0},{1,32},{2,64},{3,96},{4,128},{5,160},{6,192},{7,224},{32,1},... | collective-permute-start | bytes 393224 | tf_op jit(solution)/shard_map/ppermute | solution.py:173
  (9 other events, 48.5 us)
Sparse Core Ops, SparseCore 0:
  10.8 101.5 all-gather.6
  114.2 88.0 all-gather.8
  204.9 88.4 all-gather.10
Sparse Core Ops, SparseCore 1:
  65.7 43.7 reduce-scatter.1

commit v2 on v1

v2 whole, which is shorter than its diff:
```python
import jax
import jax.numpy as jnp
from jax import lax
from jax.experimental import pallas as pl
from jax.experimental.pallas import tpu as pltpu
from jax.sharding import Mesh
from jax.sharding import PartitionSpec as P

LR = 3584
NRHS = 512
BF = jnp.bfloat16
F32 = jnp.float32
E_STEP = 16
UNROLL = 8

Z, C, H, L, X = "z", "c", "h", "l", "x"
FRONT = (H, L, X)
PAIR = (L, X)


def dot_t(a, b):
    return lax.dot_general(a, b, (((1,), (1,)), ((), ())), preferred_element_type=F32)


def dot(a, b):
    return lax.dot_general(a, b, (((1,), (0,)), ((), ())), preferred_element_type=F32)


def exchange(chunks, axes):
    return lax.all_to_all(chunks, axes, split_axis=0, concat_axis=0, tiled=True)


def reduce_chunks(chunks, axes):
    return jnp.sum(exchange(chunks.astype(BF), axes).astype(F32), axis=0)


def gather_chunks(chunk, axes, count):
    return exchange(jnp.broadcast_to(chunk[None], (count,) + chunk.shape), axes)


def pair_up(is_first, own, other, axis):
    first = jnp.where(is_first, own, other)
    second = jnp.where(is_first, other, own)
    return jnp.concatenate([first, second], axis)


def loads_kernel(block_ref, var_ref, dofs_ref, table_ref, sens_ref, out_ref, total):
    step = pl.program_id(0)

    @pl.when(step == 0)
    def _():
        total[...] = jnp.zeros_like(total)

    row_at = lax.broadcasted_iota(jnp.int32, (128, 24), 0)
    lane_at = lax.broadcasted_iota(jnp.int32, (128, 128), 1)

    def group(index, carry):
        first = index * UNROLL
        spread = []
        for k in range(UNROLL):
            at = first + k
            start = block_ref[step * E_STEP + at] * 128
            hits = (dofs_ref[at] == row_at + start).astype(F32).astype(BF)
            spread.append(jnp.dot(hits, table_ref[at], preferred_element_type=F32))
        for k in range(UNROLL):
            at = first + k
            start = pl.multiple_of(block_ref[step * E_STEP + at] * 128, 128)
            rows = pl.ds(start, 128)
            part = jnp.dot(spread[k][:, :24].astype(BF), sens_ref[at], preferred_element_type=F32)
            total[rows, :] += part
            var = var_ref[step * E_STEP + at]
            tile = pl.ds(pl.multiple_of((var // 128) * 128, 128), 128)
            drive = spread[k][:, 24:25] + spread[k][:, 25:26] + spread[k][:, 26:27]
            total[rows, tile] += jnp.where(lane_at == var % 128, drive, 0.0)
        return carry

    lax.fori_loop(0, E_STEP // UNROLL, group, 0)

    @pl.when(step == pl.num_programs(0) - 1)
    def _():
        def turn(block, carry):
            rows = pl.ds(pl.multiple_of(block * 128, 128), 128)
            for q in range(4):
                tile = total[rows, q * 128 : q * 128 + 128].T.astype(BF)
                for k in range(4):
                    out_ref[k % 2, 2 * q + k // 2, :, rows] = tile[k * 32 : k * 32 + 32]
            return carry

        lax.fori_loop(0, LR // 128, turn, 0)


def form_loads(tables, derivs, disps, sens_block, variables, places):
    drive = jnp.sum(derivs.astype(F32) * disps.astype(F32)[None], axis=1)
    high = lax.reduce_precision(drive, 8, 7)
    middle = lax.reduce_precision(drive - high, 8, 7)
    low = drive - high - middle
    extra = -jnp.stack([high, middle, low], 1).astype(BF)
    fill = jnp.zeros((24, 5, 128), BF)
    table = jnp.concatenate([-tables, extra, fill], 1).transpose(2, 0, 1)
    blocks = jnp.minimum(jnp.min(places, axis=0) // 128, LR // 128 - 1)
    dofs = places.T[:, None, :]
    smem = pl.BlockSpec(memory_space=pltpu.SMEM)
    return pl.pallas_call(
        loads_kernel,
        grid=(128 // E_STEP,),
        in_specs=[
            smem,
            smem,
            pl.BlockSpec((E_STEP, 1, 24), lambda i: (i, 0, 0)),
            pl.BlockSpec((E_STEP, 24, 32), lambda i: (i, 0, 0)),
            pl.BlockSpec((E_STEP, 24, NRHS), lambda i: (i, 0, 0)),
        ],
        out_specs=pl.BlockSpec((2, 8, 32, LR), lambda i: (0, 0, 0, 0)),
        out_shape=jax.ShapeDtypeStruct((2, 8, 32, LR), BF),
        scratch_shapes=[pltpu.VMEM((LR, NRHS), F32)],
        cost_estimate=pl.CostEstimate(flops=800_000_000, bytes_accessed=8_000_000, transcendentals=0),
        name="loads",
    )(blocks, variables, dofs, table, sens_block)


def body(
    elem_mat,
    elem_deriv,
    elem_disp,
    elem_sens,
    design_var,
    dof_rows,
    inverse_factor,
    coupling,
    front_sizes,
):
    z = lax.axis_index(Z)
    c = lax.axis_index(C)
    h = lax.axis_index(H)
    l = lax.axis_index(L)
    x = lax.axis_index(X)
    core_swap = [(0, 1), (1, 0)]

    w_own, g_own = inverse_factor, coupling
    w_other = lax.ppermute(w_own, C, core_swap)
    g_other = lax.ppermute(g_own, C, core_swap)

    def turned(value):
        return jnp.where(c == 0, value, jnp.concatenate([value[:, 512:], value[:, :512]], 1))

    count = lax.iota(jnp.int32, 1024)
    block_rows = z * 1024 + jnp.where(c == 0, count, count ^ 512)

    def mask_of(front, rows):
        size = lax.dynamic_index_in_dim(front_sizes, front, 0, keepdims=False)
        return (rows < size).astype(F32)[None, :]

    place = l * 4 + x
    mask0 = mask_of(h * 2 + l, block_rows)
    mask0f = mask_of(h * 2 + l, x * 2048 + lax.iota(jnp.int32, 2048))
    mask1 = mask_of(4 + h, block_rows)
    mask1f = mask_of(4 + h, place * 1024 + count)
    mask2 = mask_of(6, block_rows)
    mask2f = mask_of(6, h * 4096 + place * 512 + lax.iota(jnp.int32, 512))

    def times_w(rhs, first, last):
        return dot_t(rhs[:, :512], w_own[first:last]) + dot_t(rhs[:, 512:], w_other[first:last])

    def times_wt(back, first, last):
        parts = [dot(back, w[first:last]).astype(BF) for w in (w_own, w_other)]
        return jnp.concatenate(parts, 1)

    def times_g(y, first, last):
        parts = [dot_t(y, g[:, first:last]).astype(BF) for g in (g_own, g_other)]
        return jnp.concatenate(parts, 1)

    def times_gt(parent, first, last):
        return dot(parent[:, :512], g_own[:, first:last]) + dot(parent[:, 512:], g_other[:, first:last])

    def by_front(value):
        return value.reshape(8, 2, 16, 1024).transpose(1, 0, 2, 3).reshape(16, 16, 1024)

    def from_front(value):
        return value.reshape(2, 8, 16, 1024).transpose(1, 0, 2, 3).reshape(256, 1024)

    halves = form_loads(elem_mat, elem_deriv, elem_disp, elem_sens, design_var, dof_rows)
    halves = exchange(halves, C).astype(F32)
    half = halves[0] + halves[1]
    top = exchange(half[:, :, :2048].astype(BF).reshape(4, 64, 2048), X)
    top = top.reshape(4, 64, 2, 1024).transpose(0, 2, 1, 3).reshape(8, 64, 1024)
    load0 = turned(reduce_chunks(top, Z))

    rest = lax.psum_scatter(half[:, :, 2048:], Z, scatter_dimension=0, tiled=True)[0]
    turn = [(zz * 8 + ss, ss * 8 + zz) for zz in range(8) for ss in range(8)]
    load1 = turned(lax.ppermute(rest[:, :1024], (Z, L, X), turn))
    rest2 = rest[:, 1024:].reshape(2, 16, 512)
    is_even = (x & 1) == 0
    got = []
    for k in range(2):
        sent = jnp.where(is_even, rest2[k], rest2[1 - k])
        perm = [
            (zz * 16 + ff, (ff >> 1) * 16 + ((ff & 1) ^ k) * 8 + zz)
            for zz in range(8)
            for ff in range(16)
        ]
        got.append(lax.ppermute(sent, (Z, H, L, X), perm))
    load2 = pair_up((h ^ c) == 0, got[0], got[1], 1)

    rhs0 = gather_chunks((mask0 * load0).astype(BF), X, 4).reshape(256, 1024)
    y0 = mask0f * reduce_chunks(times_w(rhs0, 0, 2048).reshape(8, 32, 2048), Z)
    y0_all = gather_chunks(y0.astype(BF), Z, 8).reshape(256, 2048)
    acc0 = reduce_chunks(times_g(y0_all, 0, 2048).reshape(8, 32, 1024), PAIR)

    rhs1 = gather_chunks((mask1 * (load1 - acc0)).astype(BF), PAIR, 8).reshape(256, 1024)
    y1 = mask1f * reduce_chunks(times_w(rhs1, 2048, 3072).reshape(8, 32, 1024), Z)
    y1_all = gather_chunks(y1.astype(BF), Z, 8).reshape(256, 1024)
    acc1 = reduce_chunks(by_front(times_g(y1_all, 2048, 3072)), FRONT)

    rhs2 = from_front(gather_chunks((mask2 * (load2 - acc1)).astype(BF), FRONT, 16))
    y2 = mask2f * reduce_chunks(times_w(rhs2, 3072, 3584).reshape(8, 32, 512), Z)
    back2 = gather_chunks(y2.astype(BF), Z, 8).reshape(256, 512)
    x2 = mask2 * reduce_chunks(by_front(times_wt(back2, 3072, 3584)), FRONT)
    got = []
    for k in range(2):
        sent = jnp.where((h ^ k ^ c) == 0, x2[:, :512], x2[:, 512:])
        perm = [
            (zz * 16 + ff, (ff & 7) * 16 + 2 * zz + ((ff >> 3) ^ k))
            for zz in range(8)
            for ff in range(16)
        ]
        got.append(lax.ppermute(sent, (Z, H, L, X), perm))
    out2 = pair_up(is_even, got[0], got[1], 0)
    x2_all = from_front(gather_chunks(x2.astype(BF), FRONT, 16))

    z1 = y1 - reduce_chunks(times_gt(x2_all, 2048, 3072).reshape(8, 32, 1024), Z)
    back1 = gather_chunks((mask1f * z1).astype(BF), Z, 8).reshape(256, 1024)
    x1 = mask1 * reduce_chunks(times_wt(back1, 2048, 3072).reshape(8, 32, 1024), PAIR)
    out1 = lax.ppermute(turned(x1), (Z, L, X), turn)
    x1_all = gather_chunks(x1.astype(BF), PAIR, 8).reshape(256, 1024)

    z0 = y0 - reduce_chunks(times_gt(x1_all, 0, 2048).reshape(8, 32, 2048), Z)
    back0 = gather_chunks((mask0f * z0).astype(BF), Z, 8).reshape(256, 2048)
    x0 = mask0 * reduce_chunks(times_wt(back0, 0, 2048).reshape(4, 64, 1024), X)
    x0 = turned(x0).reshape(2, 32, 1024)
    got = []
    for k in range(2):
        sent = jnp.where(((z & 1) ^ k) == 0, x0[0], x0[1])
        perm = [
            (zz * 4 + xx, (2 * xx + ((zz & 1) ^ k)) * 4 + (zz >> 1))
            for zz in range(8)
            for xx in range(4)
        ]
        got.append(lax.ppermute(sent, (Z, X), perm))
    out0 = pair_up((z & 1) == 0, got[0], got[1], 1)
    return jnp.concatenate([out0, out1, out2], 1).T


def solution(mesh):
    fine = Mesh(mesh.devices.reshape(8, 2, 2, 2, 4), (Z, C, H, L, X))
    elem, front = (Z, C), (H, L, X)
    both = elem + front
    return jax.shard_map(
        body,
        mesh=fine,
        in_specs=(
            P(None, None, both),
            P(None, None, both),
            P(None, both),
            P(both, None, None),
            P(both),
            P(None, both),
            P(front, elem),
            P(elem, front),
            P(),
        ),
        out_specs=P(front, elem),
        check_vma=False,
    )
```

time: 564 us -> 562 us (level)
  matrix products: 78.1 us -> 34.1 us
  blocking collectives: 181 us -> 214 us
  Pallas kernels: 0 us -> 21.6 us
  waiting for transfers between devices: 119 us -> 140 us
  local copies, waits for them, and re-layouts: 33.8 us -> 13.2 us
  other arithmetic: 42.8 us -> 26.2 us
    all_to_all x10 -> x13, blocking collectives: 181 us -> 214 us  [exchange(): return lax.all_to_all(chunks, axes, split_axis=0, concat_axis=0, tiled=True)]
    dot_general x16 -> x10, matrix products: 51.4 us -> 18.4 us  [dot_t(): lax.dot_general(a, b, (((1,), (1,)), ((), ())), preferred_element_type=F32)]
    all_to_all x7 -> x10, waiting for transfers between devices: 98.5 us -> 124 us  [exchange(): return lax.all_to_all(chunks, axes, split_axis=0, concat_axis=0, tiled=True)]
    scatter-add x1 -> x0, other arithmetic: 22.5 us -> none  [form_loads(): term_rows.at[places.T.reshape(-1)]]
    pallas_call x0 -> x1, Pallas kernels: none -> 21.6 us  [form_loads(): pl.pallas_call(loads_kernel, grid=(128 // E_STEP,), in_specs=[smem, smem,...]
    slice x7, local copies, waits for them, and re-layouts: 12.5 us -> 2.21 us  [the longest x1 1.15 us: body(): top = exchange(half[:, :, :2048].astype(BF).reshape(4, 64, 2048), X)]
    ppermute x2, starting transfers between devices: 10.6 us -> 2.06 us  [body(): got.append(lax.ppermute(sent, (Z, X), perm))]
    all_to_all x7 -> x10, starting transfers between devices: 43.3 us -> 51 us  [exchange(): return lax.all_to_all(chunks, axes, split_axis=0, concat_axis=0, tiled=True)]
  transfers between devices with their start and end apart: 23 -> 21, of which waited for: 12 -> 12; matrix products, arithmetic and copies ran while one was open for 22% -> 4% of each run, Pallas kernels for 0% -> 0%
where the time goes in v2:
time: 562 us; the launch traced here: 554 us
  blocking collectives  214 us (38%)
  waiting for transfers between devices  140 us (25%)
  starting transfers between devices  90.1 us (16%)
  matrix products  34.1 us (6%)
  other arithmetic  26.2 us (5%)
  Pallas kernels  21.6 us (4%)
  between operations  14.1 us (3%)
  local copies, waits for them, and re-layouts  13.2 us (2%)
    all_to_all x13, blocking collectives, exchange(): return lax.all_to_all(chunks, axes, split_axis=0, concat_axis=0, tiled=True)  214 us
    all_to_all x10, waiting for transfers between devices, exchange(): return lax.all_to_all(chunks, axes, split_axis=0, concat_axis=0, tiled=True)  124 us
    all_to_all x10, starting transfers between devices, exchange(): return lax.all_to_all(chunks, axes, split_axis=0, concat_axis=0, tiled=True)  51 us
    pallas_call x1, Pallas kernels, form_loads(): pl.pallas_call(loads_kernel, grid=(128 // E_STEP,), in_specs=[smem, smem,...  21.6 us
    ppermute x4, starting transfers between devices, body(): got.append(lax.ppermute(sent, (Z, H, L, X), perm))  19.3 us
    dot_general x10, matrix products, dot_t(): lax.dot_general(a, b, (((1,), (1,)), ((), ())), preferred_element_type=F32)  18.4 us
    dot_general x10, matrix products, dot(): lax.dot_general(a, b, (((1,), (0,)), ((), ())), preferred_element_type=F32)  15.7 us
    ppermute x1, starting transfers between devices, body(): out1 = lax.ppermute(turned(x1), (Z, L, X), turn)  13.9 us
  transfers between devices with their start and end apart: 21, of which 12 were waited for; matrix products, arithmetic and copies ran while one was open for 4% of the time, Pallas kernels for 0%

profile of v2, /device:TPU:8, one launch (start us, length us, event | category | flops | bytes accessed | tf_op | source)
XLA Modules:
  0.0 553.8 jit_solution(4623776538799231855)
XLA Ops:
  14.2 21.6 %loads.1 = bf16[2,8,32,3584]{3,2,1,0:T(8,128)(2,1)} custom-call(s32[128]{0:T(128)} %fusion.74.block_ref, s32[128]{0:T(128)} %var_ref.1, s32[128,1,24]{2,1,0:T(1,128)} %bitcast.91, bf16[128,24,32]{2,1,0:T(8,128)(2,1)} %maximum_bitcast_fusion.table_ref, bf16[128,24,512]{2,1,0:T(8,128)(2,1)} %sens_ref.1), custom_call_target="tpu_custom_call" | custom-call | flops 800000000 | bytes 8000000 | tf_op jit(solution)/shard_map/loads/pallas_call | solution.py:103
  35.8 8.0 %all_to_all.115 = bf16[2,8,32,3584]{3,2,1,0:T(8,128)(2,1)S(1)} all-to-all(bf16[2,8,32,3584]{3,2,1,0:T(8,128)(2,1)} %loads.1), channel_id=1, replica_groups=mesh['z'=8,'c'=2,'h'=2,'l'=2,'x'=4] {'c'}, dimensions={0} | all-to-all | bytes 7340032 | tf_op jit(solution)/shard_map/all_to_all | solution.py:30
  48.2 4.2 all-to-all-start.1
  52.4 15.4 %all-to-all-done.1 = bf16[4,64,2048]{2,1,0:T(8,128)(2,1)S(1)} async-done(((bf16[4,64,2048]{2,1,0:T(8,128)(2,1)}), bf16[4,64,2048]{2,1,0:T(8,128)(2,1)S(1)}, u32[]{:S(2)}, u32[]{:S(2)}) %all-to-all-start.1) | async-done | bytes 1048608 | tf_op jit(solution)/shard_map/all_to_all | solution.py:30
  69.0 8.4 %all-to-all-start.2 = ((bf16[8,64,1024]{2,1,0:T(8,128)(2,1)}), bf16[8,64,1024]{2,1,0:T(8,128)(2,1)S(1)}, u32[]{:S(2)}, u32[]{:S(2)}) async-start(bf16[8,64,1024]{2,1,0:T(8,128)(2,1)} %bitcast.7), calls=%async_computation.2 | async-start | bytes 2097152 | tf_op jit(solution)/shard_map/all_to_all | solution.py:30
  78.8 26.5 %all-to-all-done.2 = bf16[8,64,1024]{2,1,0:T(8,128)(2,1)S(1)} async-done(((bf16[8,64,1024]{2,1,0:T(8,128)(2,1)}), bf16[8,64,1024]{2,1,0:T(8,128)(2,1)S(1)}, u32[]{:S(2)}, u32[]{:S(2)}) %all-to-all-start.2) | async-done | bytes 1048608 | tf_op jit(solution)/shard_map/all_to_all | solution.py:30
  105.7 12.6 %all_to_all.116 = bf16[4,64,1024]{2,1,0:T(8,128)(2,1)S(1)} all-to-all(bf16[4,64,1024]{2,1,0:T(8,128)(2,1)S(1)} %broadcast_in_dim.26), channel_id=1, replica_groups=mesh['z'=8,'c'=2,'h'=2,'l'=2,'x'=4] {'x'}, dimensions={0} | all-to-all | bytes 1048576 | tf_op jit(solution)/shard_map/all_to_all | solution.py:30
  129.5 29.4 %all-to-all-done.4 = bf16[8,32,2048]{2,1,0:T(8,128)(2,1)S(1)} async-done(((bf16[8,32,2048]{2,1,0:T(8,128)(2,1)}), bf16[8,32,2048]{2,1,0:T(8,128)(2,1)S(1)}, u32[]{:S(2)}, u32[]{:S(2)}) %all-to-all-start.4) | async-done | bytes 1048608 | tf_op jit(solution)/shard_map/all_to_all | solution.py:30
  159.2 34.3 %all_to_all.117 = bf16[8,32,2048]{2,1,0:T(8,128)(2,1)S(1)} all-to-all(bf16[8,32,2048]{2,1,0:T(8,128)(2,1)S(1)} %broadcast_in_dim.27), channel_id=1, replica_groups=mesh['z'=8,'c'=2,'h'=2,'l'=2,'x'=4] {'z'}, dimensions={0} | all-to-all | bytes 2097152 | tf_op jit(solution)/shard_map/all_to_all | solution.py:30
  206.9 7.4 %collective-permute-done.1 = f32[32,1024]{1,0:T(8,128)S(1)} collective-permute-done((f32[32,1024]{1,0:T(8,128)S(1)}, f32[32,1024]{1,0:T(8,128)S(1)}, u32[]{:S(2)}, u32[]{:S(2)}) %collective-permute-start.1) | collective-permute-done | bytes 131104 | tf_op jit(solution)/shard_map/ppermute | solution.py:190
  214.5 20.4 %all_to_all.118 = bf16[8,32,1024]{2,1,0:T(8,128)(2,1)S(1)} all-to-all(bf16[8,32,1024]{2,1,0:T(8,128)(2,1)S(1)} %broadcast_in_dim.28), channel_id=1, replica_groups=mesh['z'=8,'c'=2,'h'=2,'l'=2,'x'=4] {'l','x'}, dimensions={0} | all-to-all | bytes 1048576 | tf_op jit(solution)/shard_map/all_to_all | solution.py:30
  244.7 15.1 %all-to-all-done.8 = bf16[8,32,1024]{2,1,0:T(8,128)(2,1)} async-done(((bf16[8,32,1024]{2,1,0:T(8,128)(2,1)}), bf16[8,32,1024]{2,1,0:T(8,128)(2,1)}, u32[]{:S(2)}, u32[]{:S(2)}) %all-to-all-start.8) | async-done | bytes 524320 | tf_op jit(solution)/shard_map/all_to_all | solution.py:30
  262.5 4.3 all-to-all-start.9
  266.8 14.9 %all-to-all-done.9 = bf16[8,32,1024]{2,1,0:T(8,128)(2,1)} async-done(((bf16[8,32,1024]{2,1,0:T(8,128)(2,1)}), bf16[8,32,1024]{2,1,0:T(8,128)(2,1)}, u32[]{:S(2)}, u32[]{:S(2)}) %all-to-all-start.9) | async-done | bytes 524320 | tf_op jit(solution)/shard_map/all_to_all | solution.py:30
  286.0 7.7 %all-to-all-start.10 = ((bf16[16,16,1024]{2,1,0:T(8,128)(2,1)}), bf16[16,16,1024]{2,1,0:T(8,128)(2,1)}, u32[]{:S(2)}, u32[]{:S(2)}) async-start(bf16[16,16,1024]{2,1,0:T(8,128)(2,1)} %bitcast.65), calls=%async_computation.11 | async-start | bytes 1048576 | tf_op jit(solution)/shard_map/all_to_all | solution.py:30
  297.2 5.0 collective-permute-start.4
  311.9 15.0 %all_to_all.119 = bf16[16,16,1024]{2,1,0:T(8,128)(2,1)S(1)} all-to-all(bf16[16,16,1024]{2,1,0:T(8,128)(2,1)S(1)} %broadcast_in_dim.30), channel_id=1, replica_groups=mesh['z'=8,'c'=2,'h'=2,'l'=2,'x'=4] {'h','l','x'}, dimensions={0} | all-to-all | bytes 1048576 | tf_op jit(solution)/shard_map/all_to_all | solution.py:30
  330.5 6.1 %all-to-all-start.12 = ((bf16[8,32,512]{2,1,0:T(8,128)(2,1)}), bf16[8,32,512]{2,1,0:T(8,128)(2,1)}, u32[]{:S(2)}, u32[]{:S(2)}) async-start(bf16[8,32,512]{2,1,0:T(8,128)(2,1)} %bitcast.88), calls=%async_computation.13 | async-start | bytes 524288 | tf_op jit(solution)/shard_map/all_to_all | solution.py:30
  337.8 9.3 %all-to-all-done.12 = bf16[8,32,512]{2,1,0:T(8,128)(2,1)} async-done(((bf16[8,32,512]{2,1,0:T(8,128)(2,1)}), bf16[8,32,512]{2,1,0:T(8,128)(2,1)}, u32[]{:S(2)}, u32[]{:S(2)}) %all-to-all-start.12) | async-done | bytes 262176 | tf_op jit(solution)/shard_map/all_to_all | solution.py:30
  348.8 12.9 %all_to_all.120 = bf16[8,32,512]{2,1,0:T(8,128)(2,1)S(1)} all-to-all(bf16[8,32,512]{2,1,0:T(8,128)(2,1)S(1)} %broadcast_in_dim.31), channel_id=1, replica_groups=mesh['z'=8,'c'=2,'h'=2,'l'=2,'x'=4] {'z'}, dimensions={0} | all-to-all | bytes 524288 | tf_op jit(solution)/shard_map/all_to_all | solution.py:30
  364.5 13.3 %all_to_all.121 = bf16[16,16,1024]{2,1,0:T(8,128)(2,1)S(1)} all-to-all(bf16[16,16,1024]{2,1,0:T(8,128)(2,1)S(1)} %bitcast.72), channel_id=1, replica_groups=mesh['z'=8,'c'=2,'h'=2,'l'=2,'x'=4] {'h','l','x'}, dimensions={0} | all-to-all | bytes 1048576 | tf_op jit(solution)/shard_map/all_to_all | solution.py:30
  378.6 12.9 %all_to_all.122 = bf16[16,16,1024]{2,1,0:T(8,128)(2,1)S(1)} all-to-all(bf16[16,16,1024]{2,1,0:T(8,128)(2,1)S(1)} %broadcast_in_dim.32), channel_id=1, replica_groups=mesh['z'=8,'c'=2,'h'=2,'l'=2,'x'=4] {'h','l','x'}, dimensions={0} | all-to-all | bytes 1048576 | tf_op jit(solution)/shard_map/all_to_all | solution.py:30
  393.7 17.5 %all_to_all.123 = bf16[8,32,1024]{2,1,0:T(8,128)(2,1)S(1)} all-to-all(bf16[8,32,1024]{2,1,0:T(8,128)(2,1)S(1)} %bitcast.79), channel_id=1, replica_groups=mesh['z'=8,'c'=2,'h'=2,'l'=2,'x'=4] {'z'}, dimensions={0} | all-to-all | bytes 1048576 | tf_op jit(solution)/shard_map/all_to_all | solution.py:30
  411.4 17.2 %all_to_all.124 = bf16[8,32,1024]{2,1,0:T(8,128)(2,1)S(1)} all-to-all(bf16[8,32,1024]{2,1,0:T(8,128)(2,1)S(1)} %broadcast_in_dim.33), channel_id=1, replica_groups=mesh['z'=8,'c'=2,'h'=2,'l'=2,'x'=4] {'z'}, dimensions={0} | all-to-all | bytes 1048576 | tf_op jit(solution)/shard_map/all_to_all | solution.py:30
  431.9 11.8 %all_to_all.125 = bf16[8,32,1024]{2,1,0:T(8,128)(2,1)S(1)} all-to-all(bf16[8,32,1024]{2,1,0:T(8,128)(2,1)S(1)} %bitcast.70), channel_id=1, replica_groups=mesh['z'=8,'c'=2,'h'=2,'l'=2,'x'=4] {'l','x'}, dimensions={0} | all-to-all | bytes 1048576 | tf_op jit(solution)/shard_map/all_to_all | solution.py:30
  443.9 11.2 %all_to_all.126 = bf16[8,32,1024]{2,1,0:T(8,128)(2,1)S(1)} all-to-all(bf16[8,32,1024]{2,1,0:T(8,128)(2,1)S(1)} %broadcast_in_dim.34), channel_id=1, replica_groups=mesh['z'=8,'c'=2,'h'=2,'l'=2,'x'=4] {'l','x'}, dimensions={0} | all-to-all | bytes 1048576 | tf_op jit(solution)/shard_map/all_to_all | solution.py:30
  458.2 27.0 %all_to_all.127 = bf16[8,32,2048]{2,1,0:T(8,128)(2,1)S(1)} all-to-all(bf16[8,32,2048]{2,1,0:T(8,128)(2,1)S(1)} %bitcast.64), channel_id=1, replica_groups=mesh['z'=8,'c'=2,'h'=2,'l'=2,'x'=4] {'z'}, dimensions={0} | all-to-all | bytes 2097152 | tf_op jit(solution)/shard_map/all_to_all | solution.py:30
  490.1 8.6 %collective-permute-start.8 = (f32[16,512]{1,0:T(8,128)S(1)}, f32[16,512]{1,0:T(8,128)S(1)}, u32[]{:S(2)}, u32[]{:S(2)}) collective-permute-start(f32[16,512]{1,0:T(8,128)S(1)} %get-tuple-element.27), channel_id=1, source_target_pairs={{0,0},{1,32},{2,64},{3,96},{4,128},{5,160},{6,192},{7,224},{8,1},{... | collective-permute-start | bytes 98312 | tf_op jit(solution)/shard_map/ppermute | solution.py:226
  502.3 5.3 all-to-all-done.21
  513.1 5.0 all-to-all-start.22
  518.1 8.0 %all-to-all-done.22 = bf16[4,64,1024]{2,1,0:T(8,128)(2,1)S(1)} async-done(((bf16[4,64,1024]{2,1,0:T(8,128)(2,1)}), bf16[4,64,1024]{2,1,0:T(8,128)(2,1)S(1)}, u32[]{:S(2)}, u32[]{:S(2)}) %all-to-all-start.22) | async-done | bytes 524320 | tf_op jit(solution)/shard_map/all_to_all | solution.py:30
  528.4 13.9 %collective-permute-start.7 = (f32[32,1024]{1,0:T(8,128)S(1)}, f32[32,1024]{1,0:T(8,128)S(1)}, u32[]{:S(2)}, u32[]{:S(2)}) collective-permute-start(f32[32,1024]{1,0:T(8,128)S(1)} %maximum_select_fusion.3), channel_id=1, source_target_pairs={{0,0},{1,32},{2,64},{3,96},{4,128},{5,160},{6,192},{7,224},{32,1},... | collective-permute-start | bytes 393224 | tf_op jit(solution)/shard_map/ppermute | solution.py:233
  (142 shorter events, 109.4 us)
Async XLA Ops:
  45.2 1.9 copy-start
  48.2 19.6 %all-to-all-start.1 = ((bf16[4,64,2048]{2,1,0:T(8,128)(2,1)}), bf16[4,64,2048]{2,1,0:T(8,128)(2,1)S(1)}, u32[]{:S(2)}, u32[]{:S(2)}) async-start(bf16[4,64,2048]{2,1,0:T(8,128)(2,1)} %bitcast.6), calls=%async_computation.1 | async-start | bytes 2097152 | tf_op jit(solution)/shard_map/all_to_all | solution.py:30
  52.4 25.0 %copy-start.7 = (s32[7]{0:T(128)S(1)}, s32[7]{0:T(128)}, u32[]{:S(2)}) copy-start(s32[7]{0:T(128)} %param.17) | copy-start | bytes 88
  52.4 66.6 %collective-permute-start = (bf16[3584,512]{1,0:T(8,128)(2,1)}, bf16[3584,512]{1,0:T(8,128)(2,1)}, u32[]{:S(2)}, u32[]{:S(2)}) collective-permute-start(bf16[3584,512]{1,0:T(8,128)(2,1)} %param.15), channel_id=1, source_target_pairs={{0,16},{16,0},{1,17},{17,1},{2,18},{18,2},{3,19},{19,3},{4,20},{20... | collective-permute-start | bytes 11010056 | tf_op jit(solution)/shard_map/ppermute | solution.py:140
  69.0 36.3 %all-to-all-start.2 = ((bf16[8,64,1024]{2,1,0:T(8,128)(2,1)}), bf16[8,64,1024]{2,1,0:T(8,128)(2,1)S(1)}, u32[]{:S(2)}, u32[]{:S(2)}) async-start(bf16[8,64,1024]{2,1,0:T(8,128)(2,1)} %bitcast.7), calls=%async_computation.2 | async-start | bytes 2097152 | tf_op jit(solution)/shard_map/all_to_all | solution.py:30
  105.4 12.9 %copy-start.1 = (bf16[3584,512]{1,0:T(8,128)(2,1)S(1)}, bf16[3584,512]{1,0:T(8,128)(2,1)}, u32[]{:S(2)}) copy-start(bf16[3584,512]{1,0:T(8,128)(2,1)} %param.15) | copy-start | bytes 11010052
  122.4 36.5 %all-to-all-start.4 = ((bf16[8,32,2048]{2,1,0:T(8,128)(2,1)}), bf16[8,32,2048]{2,1,0:T(8,128)(2,1)S(1)}, u32[]{:S(2)}, u32[]{:S(2)}) async-start(bf16[8,32,2048]{2,1,0:T(8,128)(2,1)} %bitcast.9), calls=%async_computation.4 | async-start | bytes 2097152 | tf_op jit(solution)/shard_map/all_to_all | solution.py:30
  126.0 75.6 %reduce-scatter.2.cloned.1.call-start = ((), (), s32[]{:S(2)}) async-start(), calls=%async_computation.24 | async-start | bytes 1769472 | tf_op jit(solution)/shard_map/reduce_scatter | solution.py:188
  126.0 68.2 %collective-permute-start.2 = (bf16[512,3072]{1,0:T(8,128)(2,1)}, bf16[512,3072]{1,0:T(8,128)(2,1)}, u32[]{:S(2)}, u32[]{:S(2)}) collective-permute-start(bf16[512,3072]{1,0:T(8,128)(2,1)} %param.16), channel_id=1, source_target_pairs={{0,16},{16,0},{1,17},{17,1},{2,18},{18,2},{3,19},{19,3},{4,20},{20... | collective-permute-start | bytes 9437192 | tf_op jit(solution)/shard_map/ppermute | solution.py:141
  159.0 34.6 %copy-start.2 = (bf16[512,3072]{1,0:T(8,128)(2,1)S(1)}, bf16[512,3072]{1,0:T(8,128)(2,1)}, u32[]{:S(2)}) copy-start(bf16[512,3072]{1,0:T(8,128)(2,1)} %param.16) | copy-start | bytes 9437188
  197.5 16.8 %all-to-all-start.6 = ((bf16[8,32,1024]{2,1,0:T(8,128)(2,1)}), bf16[8,32,1024]{2,1,0:T(8,128)(2,1)S(1)}, u32[]{:S(2)}, u32[]{:S(2)}) async-start(bf16[8,32,1024]{2,1,0:T(8,128)(2,1)} %bitcast.13), calls=%async_computation.7 | async-start | bytes 1048576 | tf_op jit(solution)/shard_map/all_to_all | solution.py:30
  202.5 11.8 %collective-permute-start.1 = (f32[32,1024]{1,0:T(8,128)S(1)}, f32[32,1024]{1,0:T(8,128)S(1)}, u32[]{:S(2)}, u32[]{:S(2)}) collective-permute-start(f32[32,1024]{1,0:T(8,128)S(1)} %slice.200), channel_id=1, source_target_pairs={{0,0},{1,32},{2,64},{3,96},{4,128},{5,160},{6,192},{7,224},{32,1},... | collective-permute-start | bytes 393224 | tf_op jit(solution)/shard_map/ppermute | solution.py:190
  236.6 45.1 %copy-start.3 = (bf16[512,3072]{1,0:T(8,128)(2,1)S(1)}, bf16[512,3072]{1,0:T(8,128)(2,1)}, u32[]{:S(2)}) copy-start(bf16[512,3072]{1,0:T(8,128)(2,1)} %param.16) | copy-start | bytes 9437188
  239.3 20.5 %all-to-all-start.8 = ((bf16[8,32,1024]{2,1,0:T(8,128)(2,1)}), bf16[8,32,1024]{2,1,0:T(8,128)(2,1)}, u32[]{:S(2)}, u32[]{:S(2)}) async-start(bf16[8,32,1024]{2,1,0:T(8,128)(2,1)} %bitcast.74), calls=%async_computation.9 | async-start | bytes 1048576 | tf_op jit(solution)/shard_map/all_to_all | solution.py:30
  262.5 19.2 %all-to-all-start.9 = ((bf16[8,32,1024]{2,1,0:T(8,128)(2,1)}), bf16[8,32,1024]{2,1,0:T(8,128)(2,1)}, u32[]{:S(2)}, u32[]{:S(2)}) async-start(bf16[8,32,1024]{2,1,0:T(8,128)(2,1)} %broadcast_in_dim.29), calls=%async_computation.10 | async-start | bytes 1048576 | tf_op jit(solution)/shard_map/all_to_all | solution.py:30
  286.0 24.0 %all-to-all-start.10 = ((bf16[16,16,1024]{2,1,0:T(8,128)(2,1)}), bf16[16,16,1024]{2,1,0:T(8,128)(2,1)}, u32[]{:S(2)}, u32[]{:S(2)}) async-start(bf16[16,16,1024]{2,1,0:T(8,128)(2,1)} %bitcast.65), calls=%async_computation.11 | async-start | bytes 1048576 | tf_op jit(solution)/shard_map/all_to_all | solution.py:30
  295.1 11.0 %collective-permute-start.3 = (f32[16,512]{1,0:T(8,128)}, f32[16,512]{1,0:T(8,128)}, u32[]{:S(2)}, u32[]{:S(2)}) collective-permute-start(f32[16,512]{1,0:T(8,128)} %get-tuple-element.19), channel_id=1, source_target_pairs={{0,0},{1,8},{2,32},{3,40},{4,64},{5,72},{6,96},{7,104},{8,128},{9,... | collective-permute-start | bytes 98312 | tf_op jit(solution)/shard_map/ppermute | solution.py:201
  297.2 11.4 %collective-permute-start.4 = (f32[16,512]{1,0:T(8,128)}, f32[16,512]{1,0:T(8,128)}, u32[]{:S(2)}, u32[]{:S(2)}) collective-permute-start(f32[16,512]{1,0:T(8,128)} %get-tuple-element.20), channel_id=1, source_target_pairs={{0,8},{1,0},{2,40},{3,32},{4,72},{5,64},{6,104},{7,96},{8,136},{9,... | collective-permute-start | bytes 98312 | tf_op jit(solution)/shard_map/ppermute | solution.py:201
  330.5 16.7 %all-to-all-start.12 = ((bf16[8,32,512]{2,1,0:T(8,128)(2,1)}), bf16[8,32,512]{2,1,0:T(8,128)(2,1)}, u32[]{:S(2)}, u32[]{:S(2)}) async-start(bf16[8,32,512]{2,1,0:T(8,128)(2,1)} %bitcast.88), calls=%async_computation.13 | async-start | bytes 524288 | tf_op jit(solution)/shard_map/all_to_all | solution.py:30
  348.8 29.1 %copy-start.6 = (f32[1024]{0:T(1024)S(1)}, f32[1024]{0:T(1024)}, u32[]{:S(2)}) copy-start(f32[1024]{0:T(1024)} %fusion.71) | copy-start | bytes 12292
  391.5 19.7 %copy-start.5 = (f32[1024]{0:T(1024)S(1)}, f32[1024]{0:T(1024)}, u32[]{:S(2)}) copy-start(f32[1024]{0:T(1024)} %fusion.72) | copy-start | bytes 12292
  485.2 4.9 copy-start.4
  486.5 21.1 %all-to-all-start.21 = ((bf16[8,32,2048]{2,1,0:T(8,128)(2,1)}), bf16[8,32,2048]{2,1,0:T(8,128)(2,1)S(1)}, u32[]{:S(2)}, u32[]{:S(2)}) async-start(bf16[8,32,2048]{2,1,0:T(8,128)(2,1)} %broadcast_in_dim.35), calls=%async_computation.22 | async-start | bytes 2097152 | tf_op jit(solution)/shard_map/all_to_all | solution.py:30
  490.1 27.9 %collective-permute-start.8 = (f32[16,512]{1,0:T(8,128)S(1)}, f32[16,512]{1,0:T(8,128)S(1)}, u32[]{:S(2)}, u32[]{:S(2)}) collective-permute-start(f32[16,512]{1,0:T(8,128)S(1)} %get-tuple-element.27), channel_id=1, source_target_pairs={{0,0},{1,32},{2,64},{3,96},{4,128},{5,160},{6,192},{7,224},{8,1},{... | collective-permute-start | bytes 98312 | tf_op jit(solution)/shard_map/ppermute | solution.py:226
  498.7 19.3 %collective-permute-start.9 = (f32[16,512]{1,0:T(8,128)S(1)}, f32[16,512]{1,0:T(8,128)S(1)}, u32[]{:S(2)}, u32[]{:S(2)}) collective-permute-start(f32[16,512]{1,0:T(8,128)S(1)} %get-tuple-element.28), channel_id=1, source_target_pairs={{0,1},{1,33},{2,65},{3,97},{4,129},{5,161},{6,193},{7,225},{8,0},{... | collective-permute-start | bytes 98312 | tf_op jit(solution)/shard_map/ppermute | solution.py:226
  513.1 13.0 %all-to-all-start.22 = ((bf16[4,64,1024]{2,1,0:T(8,128)(2,1)}), bf16[4,64,1024]{2,1,0:T(8,128)(2,1)S(1)}, u32[]{:S(2)}, u32[]{:S(2)}) async-start(bf16[4,64,1024]{2,1,0:T(8,128)(2,1)} %bitcast.38), calls=%async_computation.23 | async-start | bytes 1048576 | tf_op jit(solution)/shard_map/all_to_all | solution.py:30
  526.3 16.0 %collective-permute-start.5 = (f32[32,1024]{1,0:T(8,128)S(1)}, f32[32,1024]{1,0:T(8,128)S(1)}, u32[]{:S(2)}, u32[]{:S(2)}) collective-permute-start(f32[32,1024]{1,0:T(8,128)S(1)} %get-tuple-element.13), channel_id=1, source_target_pairs={{0,0},{1,64},{2,128},{3,192},{32,32},{33,96},{34,160},{35,224},{64... | collective-permute-start | bytes 393224 | tf_op jit(solution)/shard_map/ppermute | solution.py:248
  527.0 15.3 %collective-permute-start.6 = (f32[32,1024]{1,0:T(8,128)S(1)}, f32[32,1024]{1,0:T(8,128)S(1)}, u32[]{:S(2)}, u32[]{:S(2)}) collective-permute-start(f32[32,1024]{1,0:T(8,128)S(1)} %get-tuple-element.14), channel_id=1, source_target_pairs={{0,32},{1,96},{2,160},{3,224},{32,0},{33,64},{34,128},{35,192},{64... | collective-permute-start | bytes 393224 | tf_op jit(solution)/shard_map/ppermute | solution.py:248
  528.4 17.8 %collective-permute-start.7 = (f32[32,1024]{1,0:T(8,128)S(1)}, f32[32,1024]{1,0:T(8,128)S(1)}, u32[]{:S(2)}, u32[]{:S(2)}) collective-permute-start(f32[32,1024]{1,0:T(8,128)S(1)} %maximum_select_fusion.3), channel_id=1, source_target_pairs={{0,0},{1,32},{2,64},{3,96},{4,128},{5,160},{6,192},{7,224},{32,1},... | collective-permute-start | bytes 393224 | tf_op jit(solution)/shard_map/ppermute | solution.py:233
Sparse Core Ops, SparseCore 0:
  129.4 51.9 reduce-scatter.1

commit v3 on v2

--- a/solution.py
+++ b/solution.py
@@ -52,16 +52,25 @@
         total[...] = jnp.zeros_like(total)
 
     row_at = lax.broadcasted_iota(jnp.int32, (128, 24), 0)
-    lane_at = lax.broadcasted_iota(jnp.int32, (128, 128), 1)
+    lane_at = lax.broadcasted_iota(jnp.int32, (24, 128), 1)
 
     def group(index, carry):
         first = index * UNROLL
         spread = []
+        drives = []
         for k in range(UNROLL):
             at = first + k
             start = block_ref[step * E_STEP + at] * 128
             hits = (dofs_ref[at] == row_at + start).astype(F32).astype(BF)
-            spread.append(jnp.dot(hits, table_ref[at], preferred_element_type=F32))
+            table = table_ref[at]
+            spread.append(jnp.dot(hits, table, preferred_element_type=F32))
+            here = lane_at == var_ref[step * E_STEP + at] % 128
+            drive = 0.0
+            for p in range(2):
+                piece = table[:, 24 + p : 25 + p].astype(F32)
+                piece = jnp.where(here, piece, 0.0).astype(BF)
+                drive += jnp.dot(hits, piece, preferred_element_type=F32)
+            drives.append(drive)
         for k in range(UNROLL):
             at = first + k
             start = pl.multiple_of(block_ref[step * E_STEP + at] * 128, 128)
@@ -70,8 +79,7 @@
             total[rows, :] += part
             var = var_ref[step * E_STEP + at]
             tile = pl.ds(pl.multiple_of((var // 128) * 128, 128), 128)
-            drive = spread[k][:, 24:25] + spread[k][:, 25:26] + spread[k][:, 26:27]
-            total[rows, tile] += jnp.where(lane_at == var % 128, drive, 0.0)
+            total[rows, tile] += drives[k]
         return carry
 
     lax.fori_loop(0, E_STEP // UNROLL, group, 0)
@@ -81,7 +89,7 @@
         def turn(block, carry):
             rows = pl.ds(pl.multiple_of(block * 128, 128), 128)
             for q in range(4):
-                tile = total[rows, q * 128 : q * 128 + 128].T.astype(BF)
+                tile = total[rows, q * 128 : q * 128 + 128].astype(BF).T
                 for k in range(4):
                     out_ref[k % 2, 2 * q + k // 2, :, rows] = tile[k * 32 : k * 32 + 32]
             return carry
@@ -92,10 +100,8 @@
 def form_loads(tables, derivs, disps, sens_block, variables, places):
     drive = jnp.sum(derivs.astype(F32) * disps.astype(F32)[None], axis=1)
     high = lax.reduce_precision(drive, 8, 7)
-    middle = lax.reduce_precision(drive - high, 8, 7)
-    low = drive - high - middle
-    extra = -jnp.stack([high, middle, low], 1).astype(BF)
-    fill = jnp.zeros((24, 5, 128), BF)
+    extra = -jnp.stack([high, drive - high], 1).astype(BF)
+    fill = jnp.zeros((24, 6, 128), BF)
     table = jnp.concatenate([-tables, extra, fill], 1).transpose(2, 0, 1)
     blocks = jnp.minimum(jnp.min(places, axis=0) // 128, LR // 128 - 1)
     dofs = places.T[:, None, :]
@@ -180,12 +186,24 @@
 
     halves = form_loads(elem_mat, elem_deriv, elem_disp, elem_sens, design_var, dof_rows)
     halves = exchange(halves, C).astype(F32)
-    half = halves[0] + halves[1]
-    top = exchange(half[:, :, :2048].astype(BF).reshape(4, 64, 2048), X)
+    half = (halves[0] + halves[1]).astype(BF)
+    top = exchange(half[:, :, :2048].reshape(4, 64, 2048), X)
+
+    def halved(value, bit):
+        pairs = value.reshape(-1, 2, 32, 1536)
+        is_low = ((z >> bit) & 1) == 0
+        kept = jnp.where(is_low, pairs[:, 0], pairs[:, 1])
+        sent = jnp.where(is_low, pairs[:, 1], pairs[:, 0]).astype(BF)
+        perm = [(at, at ^ (1 << bit)) for at in range(8)]
+        return kept.astype(F32) + lax.ppermute(sent, Z, perm).astype(F32)
+
+    rest = halved(half[:, :, 2048:], 0)
+    top, rest = lax.optimization_barrier((top, rest))
     top = top.reshape(4, 64, 2, 1024).transpose(0, 2, 1, 3).reshape(8, 64, 1024)
     load0 = turned(reduce_chunks(top, Z))
-
-    rest = lax.psum_scatter(half[:, :, 2048:], Z, scatter_dimension=0, tiled=True)[0]
+    rhs0 = gather_chunks((mask0 * load0).astype(BF), X, 4).reshape(256, 1024)
+    rest = halved(halved(rest, 1), 2)[0]
+    rhs0, rest = lax.optimization_barrier((rhs0, rest))
     turn = [(zz * 8 + ss, ss * 8 + zz) for zz in range(8) for ss in range(8)]
     load1 = turned(lax.ppermute(rest[:, :1024], (Z, L, X), turn))
     rest2 = rest[:, 1024:].reshape(2, 16, 512)
@@ -201,8 +219,8 @@
         got.append(lax.ppermute(sent, (Z, H, L, X), perm))
     load2 = pair_up((h ^ c) == 0, got[0], got[1], 1)
 
-    rhs0 = gather_chunks((mask0 * load0).astype(BF), X, 4).reshape(256, 1024)
     y0 = mask0f * reduce_chunks(times_w(rhs0, 0, 2048).reshape(8, 32, 2048), Z)
+    y0, load1, load2 = lax.optimization_barrier((y0, load1, load2))
     y0_all = gather_chunks(y0.astype(BF), Z, 8).reshape(256, 2048)
     acc0 = reduce_chunks(times_g(y0_all, 0, 2048).reshape(8, 32, 1024), PAIR)
 

time: 562 us -> 531 us (0.945)
  starting transfers between devices: 90.1 us -> 106 us
  waiting for transfers between devices: 140 us -> 126 us
  between operations: 14.1 us -> 0.83 us
  blocking collectives: 214 us -> 205 us
    all_to_all x10 -> x11, waiting for transfers between devices: 124 us -> 75.1 us  [exchange(): return lax.all_to_all(chunks, axes, split_axis=0, concat_axis=0, tiled=True)]
    ppermute x0 -> x3, waiting for transfers between devices: none -> 33.3 us  [halved(): return kept.astype(F32) + lax.ppermute(sent, Z, perm).astype(F32)]
    all_to_all x13 -> x12, blocking collectives: 214 us -> 205 us  [exchange(): return lax.all_to_all(chunks, axes, split_axis=0, concat_axis=0, tiled=True)]
    ppermute x0 -> x3, starting transfers between devices: none -> 8.73 us  [halved(): return kept.astype(F32) + lax.ppermute(sent, Z, perm).astype(F32)]
    ppermute x4, waiting for transfers between devices: 5.12 us -> 12 us  [body(): got.append(lax.ppermute(sent, (Z, H, L, X), perm))]
    all_to_all x10 -> x11, starting transfers between devices: 51 us -> 54.8 us  [exchange(): return lax.all_to_all(chunks, axes, split_axis=0, concat_axis=0, tiled=True)]
  transfers between devices with their start and end apart: 21 -> 24, of which waited for: 12 -> 15; matrix products, arithmetic and copies ran while one was open for 4% -> 4% of each run, Pallas kernels for 0% -> 0%
where the time goes in v3:
time: 531 us; the launch traced here: 523 us
  blocking collectives  205 us (39%)
  waiting for transfers between devices  126 us (24%)
  starting transfers between devices  106 us (20%)
  matrix products  34.4 us (6%)
  other arithmetic  24.8 us (5%)
  Pallas kernels  17.4 us (3%)
  local copies, waits for them, and re-layouts  7.73 us (1%)
    all_to_all x12, blocking collectives, exchange(): return lax.all_to_all(chunks, axes, split_axis=0, concat_axis=0, tiled=True)  205 us
    all_to_all x11, waiting for transfers between devices, exchange(): return lax.all_to_all(chunks, axes, split_axis=0, concat_axis=0, tiled=True)  75.1 us
    all_to_all x11, starting transfers between devices, exchange(): return lax.all_to_all(chunks, axes, split_axis=0, concat_axis=0, tiled=True)  54.8 us
    ppermute x3, waiting for transfers between devices, halved(): return kept.astype(F32) + lax.ppermute(sent, Z, perm).astype(F32)  33.3 us
    ppermute x4, starting transfers between devices, body(): got.append(lax.ppermute(sent, (Z, H, L, X), perm))  21 us
    dot_general x10, matrix products, dot_t(): lax.dot_general(a, b, (((1,), (1,)), ((), ())), preferred_element_type=F32)  18.7 us
    pallas_call x1, Pallas kernels, form_loads(): pl.pallas_call(loads_kernel, grid=(128 // E_STEP,), in_specs=[smem, smem,...  17.4 us
    dot_general x10, matrix products, dot(): lax.dot_general(a, b, (((1,), (0,)), ((), ())), preferred_element_type=F32)  15.7 us
  transfers between devices with their start and end apart: 24, of which 15 were waited for; matrix products, arithmetic and copies ran while one was open for 4% of the time, Pallas kernels for 0%

profile of v3, /device:TPU:8, one launch (start us, length us, event | category | flops | bytes accessed | tf_op | source)
XLA Modules:
  0.0 523.1 jit_solution(17171303976899987959)
XLA Ops:
  7.7 17.4 %loads.1 = bf16[2,8,32,3584]{3,2,1,0:T(8,128)(2,1)} custom-call(s32[128]{0:T(128)} %fusion.76.block_ref, s32[128]{0:T(128)} %var_ref.1, s32[128,1,24]{2,1,0:T(1,128)} %bitcast.146, bf16[128,24,32]{2,1,0:T(8,128)(2,1)} %maximum_bitcast_fusion.table_ref, bf16[128,24,512]{2,1,0:T(8,128)(2,1)} %sens_ref.1), custom_call_target="tpu_custom_call" | custom-call | flops 800000000 | bytes 8000000 | tf_op jit(solution)/shard_map/loads/pallas_call | solution.py:109
  25.1 5.4 %all-to-all-start = ((bf16[2,8,32,3584]{3,2,1,0:T(8,128)(2,1)}), bf16[2,8,32,3584]{3,2,1,0:T(8,128)(2,1)}, u32[]{:S(2)}, u32[]{:S(2)}) async-start(bf16[2,8,32,3584]{3,2,1,0:T(8,128)(2,1)} %loads.1), calls=%async_computation | async-start | bytes 7340032 | tf_op jit(solution)/shard_map/all_to_all | solution.py:30
  49.8 11.0 %all-to-all-done.1 = bf16[4,64,2048]{2,1,0:T(8,128)(2,1)S(1)} async-done(((bf16[4,64,2048]{2,1,0:T(8,128)(2,1)}), bf16[4,64,2048]{2,1,0:T(8,128)(2,1)S(1)}, u32[]{:S(2)}, u32[]{:S(2)}) %all-to-all-start.1) | async-done | bytes 1048608 | tf_op jit(solution)/shard_map/all_to_all | solution.py:30
  61.9 7.6 %all-to-all-start.2 = ((bf16[8,64,1024]{2,1,0:T(8,128)(2,1)}), bf16[8,64,1024]{2,1,0:T(8,128)(2,1)S(1)}, u32[]{:S(2)}, u32[]{:S(2)}) async-start(bf16[8,64,1024]{2,1,0:T(8,128)(2,1)} %bitcast.10), calls=%async_computation.2 | async-start | bytes 2097152 | tf_op jit(solution)/shard_map/all_to_all | solution.py:30
  73.8 28.7 %collective-permute-done.1 = bf16[2,32,1536]{2,1,0:T(8,128)(2,1)S(1)} collective-permute-done((bf16[2,32,1536]{2,1,0:T(8,128)(2,1)S(1)}, bf16[2,32,1536]{2,1,0:T(8,128)(2,1)S(1)}, u32[]{:S(2)}, u32[]{:S(2)}) %collective-permute-start.1) | collective-permute-done | bytes 196640 | tf_op jit(solution)/shard_map/ppermute | solution.py:198
  111.5 7.5 %all-to-all-done.3 = bf16[4,64,1024]{2,1,0:T(8,128)(2,1)S(1)} async-done(((bf16[4,64,1024]{2,1,0:T(8,128)(2,1)}), bf16[4,64,1024]{2,1,0:T(8,128)(2,1)S(1)}, u32[]{:S(2)}, u32[]{:S(2)}) %all-to-all-start.3) | async-done | bytes 524320 | tf_op jit(solution)/shard_map/all_to_all | solution.py:30
  128.6 4.7 collective-permute-start.5
  138.6 6.7 %collective-permute-start.4 = (f32[32,1024]{1,0:T(8,128)S(1)}, f32[32,1024]{1,0:T(8,128)S(1)}, u32[]{:S(2)}, u32[]{:S(2)}) collective-permute-start(f32[32,1024]{1,0:T(8,128)S(1)} %slice.189), channel_id=1, source_target_pairs={{0,0},{1,32},{2,64},{3,96},{4,128},{5,160},{6,192},{7,224},{32,1},... | collective-permute-start | bytes 393224 | tf_op jit(solution)/shard_map/ppermute | solution.py:208
  145.2 12.0 %collective-permute-done.5 = f32[16,512]{1,0:T(8,128)S(1)} collective-permute-done((f32[16,512]{1,0:T(8,128)S(1)}, f32[16,512]{1,0:T(8,128)S(1)}, u32[]{:S(2)}, u32[]{:S(2)}) %collective-permute-start.5) | collective-permute-done | bytes 32800 | tf_op jit(solution)/shard_map/ppermute | solution.py:219
  160.1 38.2 %all_to_all.115 = bf16[8,32,2048]{2,1,0:T(8,128)(2,1)S(1)} all-to-all(bf16[8,32,2048]{2,1,0:T(8,128)(2,1)S(1)} %broadcast_in_dim.27), channel_id=1, replica_groups=mesh['z'=8,'c'=2,'h'=2,'l'=2,'x'=4] {'z'}, dimensions={0} | all-to-all | bytes 2097152 | tf_op jit(solution)/shard_map/all_to_all | solution.py:30
  202.2 7.9 %all-to-all-start.6 = ((bf16[8,32,1024]{2,1,0:T(8,128)(2,1)}), bf16[8,32,1024]{2,1,0:T(8,128)(2,1)S(1)}, u32[]{:S(2)}, u32[]{:S(2)}) async-start(bf16[8,32,1024]{2,1,0:T(8,128)(2,1)} %bitcast.25), calls=%async_computation.6 | async-start | bytes 1048576 | tf_op jit(solution)/shard_map/all_to_all | solution.py:30
  210.8 6.6 %all-to-all-done.6 = bf16[8,32,1024]{2,1,0:T(8,128)(2,1)S(1)} async-done(((bf16[8,32,1024]{2,1,0:T(8,128)(2,1)}), bf16[8,32,1024]{2,1,0:T(8,128)(2,1)S(1)}, u32[]{:S(2)}, u32[]{:S(2)}) %all-to-all-start.6) | async-done | bytes 524320 | tf_op jit(solution)/shard_map/all_to_all | solution.py:30
  217.5 11.2 %all_to_all.116 = bf16[8,32,1024]{2,1,0:T(8,128)(2,1)S(1)} all-to-all(bf16[8,32,1024]{2,1,0:T(8,128)(2,1)S(1)} %broadcast_in_dim.28), channel_id=1, replica_groups=mesh['z'=8,'c'=2,'h'=2,'l'=2,'x'=4] {'l','x'}, dimensions={0} | all-to-all | bytes 1048576 | tf_op jit(solution)/shard_map/all_to_all | solution.py:30
  238.0 15.8 %all-to-all-done.8 = bf16[8,32,1024]{2,1,0:T(8,128)(2,1)} async-done(((bf16[8,32,1024]{2,1,0:T(8,128)(2,1)}), bf16[8,32,1024]{2,1,0:T(8,128)(2,1)}, u32[]{:S(2)}, u32[]{:S(2)}) %all-to-all-start.8) | async-done | bytes 524320 | tf_op jit(solution)/shard_map/all_to_all | solution.py:30
  255.0 18.1 %all_to_all.117 = bf16[8,32,1024]{2,1,0:T(8,128)(2,1)S(1)} all-to-all(bf16[8,32,1024]{2,1,0:T(8,128)(2,1)S(1)} %broadcast_in_dim.29), channel_id=1, replica_groups=mesh['z'=8,'c'=2,'h'=2,'l'=2,'x'=4] {'z'}, dimensions={0} | all-to-all | bytes 1048576 | tf_op jit(solution)/shard_map/all_to_all | solution.py:30
  276.3 5.4 %all-to-all-start.10 = ((bf16[16,16,1024]{2,1,0:T(8,128)(2,1)}), bf16[16,16,1024]{2,1,0:T(8,128)(2,1)}, u32[]{:S(2)}, u32[]{:S(2)}) async-start(bf16[16,16,1024]{2,1,0:T(8,128)(2,1)} %bitcast.118), calls=%async_computation.10 | async-start | bytes 1048576 | tf_op jit(solution)/shard_map/all_to_all | solution.py:30
  282.8 7.0 %all-to-all-done.10 = bf16[16,16,1024]{2,1,0:T(8,128)(2,1)} async-done(((bf16[16,16,1024]{2,1,0:T(8,128)(2,1)}), bf16[16,16,1024]{2,1,0:T(8,128)(2,1)}, u32[]{:S(2)}, u32[]{:S(2)}) %all-to-all-start.10) | async-done | bytes 524320 | tf_op jit(solution)/shard_map/all_to_all | solution.py:30
  291.9 13.1 %all_to_all.118 = bf16[16,16,1024]{2,1,0:T(8,128)(2,1)S(1)} all-to-all(bf16[16,16,1024]{2,1,0:T(8,128)(2,1)S(1)} %broadcast_in_dim.30), channel_id=1, replica_groups=mesh['z'=8,'c'=2,'h'=2,'l'=2,'x'=4] {'h','l','x'}, dimensions={0} | all-to-all | bytes 1048576 | tf_op jit(solution)/shard_map/all_to_all | solution.py:30
  313.7 9.3 %all-to-all-done.12 = bf16[8,32,512]{2,1,0:T(8,128)(2,1)} async-done(((bf16[8,32,512]{2,1,0:T(8,128)(2,1)}), bf16[8,32,512]{2,1,0:T(8,128)(2,1)}, u32[]{:S(2)}, u32[]{:S(2)}) %all-to-all-start.12) | async-done | bytes 262176 | tf_op jit(solution)/shard_map/all_to_all | solution.py:30
  324.7 12.9 %all_to_all.119 = bf16[8,32,512]{2,1,0:T(8,128)(2,1)S(1)} all-to-all(bf16[8,32,512]{2,1,0:T(8,128)(2,1)S(1)} %broadcast_in_dim.31), channel_id=1, replica_groups=mesh['z'=8,'c'=2,'h'=2,'l'=2,'x'=4] {'z'}, dimensions={0} | all-to-all | bytes 524288 | tf_op jit(solution)/shard_map/all_to_all | solution.py:30
  340.4 13.3 %all_to_all.120 = bf16[16,16,1024]{2,1,0:T(8,128)(2,1)S(1)} all-to-all(bf16[16,16,1024]{2,1,0:T(8,128)(2,1)S(1)} %bitcast.125), channel_id=1, replica_groups=mesh['z'=8,'c'=2,'h'=2,'l'=2,'x'=4] {'h','l','x'}, dimensions={0} | all-to-all | bytes 1048576 | tf_op jit(solution)/shard_map/all_to_all | solution.py:30
  354.5 12.9 %all_to_all.121 = bf16[16,16,1024]{2,1,0:T(8,128)(2,1)S(1)} all-to-all(bf16[16,16,1024]{2,1,0:T(8,128)(2,1)S(1)} %broadcast_in_dim.32), channel_id=1, replica_groups=mesh['z'=8,'c'=2,'h'=2,'l'=2,'x'=4] {'h','l','x'}, dimensions={0} | all-to-all | bytes 1048576 | tf_op jit(solution)/shard_map/all_to_all | solution.py:30
  369.6 17.9 %all_to_all.122 = bf16[8,32,1024]{2,1,0:T(8,128)(2,1)S(1)} all-to-all(bf16[8,32,1024]{2,1,0:T(8,128)(2,1)S(1)} %bitcast.132), channel_id=1, replica_groups=mesh['z'=8,'c'=2,'h'=2,'l'=2,'x'=4] {'z'}, dimensions={0} | all-to-all | bytes 1048576 | tf_op jit(solution)/shard_map/all_to_all | solution.py:30
  387.6 17.1 %all_to_all.123 = bf16[8,32,1024]{2,1,0:T(8,128)(2,1)S(1)} all-to-all(bf16[8,32,1024]{2,1,0:T(8,128)(2,1)S(1)} %broadcast_in_dim.33), channel_id=1, replica_groups=mesh['z'=8,'c'=2,'h'=2,'l'=2,'x'=4] {'z'}, dimensions={0} | all-to-all | bytes 1048576 | tf_op jit(solution)/shard_map/all_to_all | solution.py:30
  408.1 11.9 %all_to_all.124 = bf16[8,32,1024]{2,1,0:T(8,128)(2,1)S(1)} all-to-all(bf16[8,32,1024]{2,1,0:T(8,128)(2,1)S(1)} %bitcast.123), channel_id=1, replica_groups=mesh['z'=8,'c'=2,'h'=2,'l'=2,'x'=4] {'l','x'}, dimensions={0} | all-to-all | bytes 1048576 | tf_op jit(solution)/shard_map/all_to_all | solution.py:30
  420.1 11.2 %all_to_all.125 = bf16[8,32,1024]{2,1,0:T(8,128)(2,1)S(1)} all-to-all(bf16[8,32,1024]{2,1,0:T(8,128)(2,1)S(1)} %broadcast_in_dim.34), channel_id=1, replica_groups=mesh['z'=8,'c'=2,'h'=2,'l'=2,'x'=4] {'l','x'}, dimensions={0} | all-to-all | bytes 1048576 | tf_op jit(solution)/shard_map/all_to_all | solution.py:30
  434.4 27.6 %all_to_all.126 = bf16[8,32,2048]{2,1,0:T(8,128)(2,1)S(1)} all-to-all(bf16[8,32,2048]{2,1,0:T(8,128)(2,1)S(1)} %bitcast.117), channel_id=1, replica_groups=mesh['z'=8,'c'=2,'h'=2,'l'=2,'x'=4] {'z'}, dimensions={0} | all-to-all | bytes 2097152 | tf_op jit(solution)/shard_map/all_to_all | solution.py:30
  467.0 8.6 %collective-permute-start.11 = (f32[16,512]{1,0:T(8,128)S(1)}, f32[16,512]{1,0:T(8,128)S(1)}, u32[]{:S(2)}, u32[]{:S(2)}) collective-permute-start(f32[16,512]{1,0:T(8,128)S(1)} %get-tuple-element.41), channel_id=1, source_target_pairs={{0,0},{1,32},{2,64},{3,96},{4,128},{5,160},{6,192},{7,224},{8,1},{... | collective-permute-start | bytes 98312 | tf_op jit(solution)/shard_map/ppermute | solution.py:244
  478.7 5.8 %all-to-all-done.21 = bf16[8,32,2048]{2,1,0:T(8,128)(2,1)S(1)} async-done(((bf16[8,32,2048]{2,1,0:T(8,128)(2,1)}), bf16[8,32,2048]{2,1,0:T(8,128)(2,1)S(1)}, u32[]{:S(2)}, u32[]{:S(2)}) %all-to-all-start.21) | async-done | bytes 1048608 | tf_op jit(solution)/shard_map/all_to_all | solution.py:30
  490.0 4.9 all-to-all-start.22
  494.9 8.0 %all-to-all-done.22 = bf16[4,64,1024]{2,1,0:T(8,128)(2,1)S(1)} async-done(((bf16[4,64,1024]{2,1,0:T(8,128)(2,1)}), bf16[4,64,1024]{2,1,0:T(8,128)(2,1)S(1)}, u32[]{:S(2)}, u32[]{:S(2)}) %all-to-all-start.22) | async-done | bytes 524320 | tf_op jit(solution)/shard_map/all_to_all | solution.py:30
  505.1 13.3 %collective-permute-start.10 = (f32[32,1024]{1,0:T(8,128)S(1)}, f32[32,1024]{1,0:T(8,128)S(1)}, u32[]{:S(2)}, u32[]{:S(2)}) collective-permute-start(f32[32,1024]{1,0:T(8,128)S(1)} %maximum_select_fusion.3), channel_id=1, source_target_pairs={{0,0},{1,32},{2,64},{3,96},{4,128},{5,160},{6,192},{7,224},{32,1},... | collective-permute-start | bytes 393224 | tf_op jit(solution)/shard_map/ppermute | solution.py:251
  (153 shorter events, 123.2 us)
Async XLA Ops:
  25.1 9.5 %all-to-all-start = ((bf16[2,8,32,3584]{3,2,1,0:T(8,128)(2,1)}), bf16[2,8,32,3584]{3,2,1,0:T(8,128)(2,1)}, u32[]{:S(2)}, u32[]{:S(2)}) async-start(bf16[2,8,32,3584]{3,2,1,0:T(8,128)(2,1)} %loads.1), calls=%async_computation | async-start | bytes 7340032 | tf_op jit(solution)/shard_map/all_to_all | solution.py:30
  38.2 11.4 %collective-permute-start = (bf16[4,32,1536]{2,1,0:T(8,128)(2,1)S(1)}, bf16[4,32,1536]{2,1,0:T(8,128)(2,1)S(1)}, u32[]{:S(2)}, u32[]{:S(2)}) collective-permute-start(bf16[4,32,1536]{2,1,0:T(8,128)(2,1)S(1)} %select_bitcast_fusion), channel_id=1, source_target_pairs={{0,32},{32,0},{64,96},{96,64},{128,160},{160,128},{192,224},{224,1... | collective-permute-start | bytes 1179656 | tf_op jit(solution)/shard_map/ppermute | solution.py:198
  41.3 19.4 %all-to-all-start.1 = ((bf16[4,64,2048]{2,1,0:T(8,128)(2,1)}), bf16[4,64,2048]{2,1,0:T(8,128)(2,1)S(1)}, u32[]{:S(2)}, u32[]{:S(2)}) async-start(bf16[4,64,2048]{2,1,0:T(8,128)(2,1)} %bitcast.116), calls=%async_computation.1 | async-start | bytes 2097152 | tf_op jit(solution)/shard_map/all_to_all | solution.py:30
  45.6 75.7 %collective-permute-start.3 = (bf16[3584,512]{1,0:T(8,128)(2,1)}, bf16[3584,512]{1,0:T(8,128)(2,1)}, u32[]{:S(2)}, u32[]{:S(2)}) collective-permute-start(bf16[3584,512]{1,0:T(8,128)(2,1)} %param.15), channel_id=1, source_target_pairs={{0,16},{16,0},{1,17},{17,1},{2,18},{18,2},{3,19},{19,3},{4,20},{20... | collective-permute-start | bytes 11010056 | tf_op jit(solution)/shard_map/ppermute | solution.py:146
  49.8 22.7 %copy-start.6 = (s32[7]{0:T(128)S(1)}, s32[7]{0:T(128)}, u32[]{:S(2)}) copy-start(s32[7]{0:T(128)} %param.17) | copy-start | bytes 88
  61.9 44.4 %all-to-all-start.2 = ((bf16[8,64,1024]{2,1,0:T(8,128)(2,1)}), bf16[8,64,1024]{2,1,0:T(8,128)(2,1)S(1)}, u32[]{:S(2)}, u32[]{:S(2)}) async-start(bf16[8,64,1024]{2,1,0:T(8,128)(2,1)} %bitcast.10), calls=%async_computation.2 | async-start | bytes 2097152 | tf_op jit(solution)/shard_map/all_to_all | solution.py:30
  69.5 33.0 %collective-permute-start.1 = (bf16[2,32,1536]{2,1,0:T(8,128)(2,1)S(1)}, bf16[2,32,1536]{2,1,0:T(8,128)(2,1)S(1)}, u32[]{:S(2)}, u32[]{:S(2)}) collective-permute-start(bf16[2,32,1536]{2,1,0:T(8,128)(2,1)S(1)} %fusion.63), channel_id=1, source_target_pairs={{0,64},{32,96},{64,0},{96,32},{128,192},{160,224},{192,128},{224,1... | collective-permute-start | bytes 589832 | tf_op jit(solution)/shard_map/ppermute | solution.py:198
  102.6 8.9 %collective-permute-start.2 = (bf16[1,32,1536]{2,1,0:T(8,128)(2,1)S(1)}, bf16[1,32,1536]{2,1,0:T(8,128)(2,1)S(1)}, u32[]{:S(2)}, u32[]{:S(2)}) collective-permute-start(bf16[1,32,1536]{2,1,0:T(8,128)(2,1)S(1)} %fusion.65), channel_id=1, source_target_pairs={{0,128},{32,160},{64,192},{96,224},{128,0},{160,32},{192,64},{224,... | collective-permute-start | bytes 294920 | tf_op jit(solution)/shard_map/ppermute | solution.py:198
  107.4 11.5 %all-to-all-start.3 = ((bf16[4,64,1024]{2,1,0:T(8,128)(2,1)}), bf16[4,64,1024]{2,1,0:T(8,128)(2,1)S(1)}, u32[]{:S(2)}, u32[]{:S(2)}) async-start(bf16[4,64,1024]{2,1,0:T(8,128)(2,1)} %broadcast_in_dim.26), calls=%async_computation.3 | async-start | bytes 1048576 | tf_op jit(solution)/shard_map/all_to_all | solution.py:30
  124.6 35.2 %all-to-all-start.4 = ((bf16[8,32,2048]{2,1,0:T(8,128)(2,1)}), bf16[8,32,2048]{2,1,0:T(8,128)(2,1)S(1)}, u32[]{:S(2)}, u32[]{:S(2)}) async-start(bf16[8,32,2048]{2,1,0:T(8,128)(2,1)} %bitcast.22), calls=%async_computation.4 | async-start | bytes 2097152 | tf_op jit(solution)/shard_map/all_to_all | solution.py:30
  128.6 70.5 %collective-permute-start.7 = (bf16[512,3072]{1,0:T(8,128)(2,1)}, bf16[512,3072]{1,0:T(8,128)(2,1)}, u32[]{:S(2)}, u32[]{:S(2)}) collective-permute-start(bf16[512,3072]{1,0:T(8,128)(2,1)} %param.16), channel_id=1, source_target_pairs={{0,16},{16,0},{1,17},{17,1},{2,18},{18,2},{3,19},{19,3},{4,20},{20... | collective-permute-start | bytes 9437192 | tf_op jit(solution)/shard_map/ppermute | solution.py:147
  128.6 28.6 %collective-permute-start.5 = (f32[16,512]{1,0:T(8,128)S(1)}, f32[16,512]{1,0:T(8,128)S(1)}, u32[]{:S(2)}, u32[]{:S(2)}) collective-permute-start(f32[16,512]{1,0:T(8,128)S(1)} %get-tuple-element.33), channel_id=1, source_target_pairs={{0,0},{1,8},{2,32},{3,40},{4,64},{5,72},{6,96},{7,104},{8,128},{9,... | collective-permute-start | bytes 98312 | tf_op jit(solution)/shard_map/ppermute | solution.py:219
  133.3 23.9 %collective-permute-start.6 = (f32[16,512]{1,0:T(8,128)S(1)}, f32[16,512]{1,0:T(8,128)S(1)}, u32[]{:S(2)}, u32[]{:S(2)}) collective-permute-start(f32[16,512]{1,0:T(8,128)S(1)} %get-tuple-element.34), channel_id=1, source_target_pairs={{0,8},{1,0},{2,40},{3,32},{4,72},{5,64},{6,104},{7,96},{8,136},{9,... | collective-permute-start | bytes 98312 | tf_op jit(solution)/shard_map/ppermute | solution.py:219
  138.6 21.2 %collective-permute-start.4 = (f32[32,1024]{1,0:T(8,128)S(1)}, f32[32,1024]{1,0:T(8,128)S(1)}, u32[]{:S(2)}, u32[]{:S(2)}) collective-permute-start(f32[32,1024]{1,0:T(8,128)S(1)} %slice.189), channel_id=1, source_target_pairs={{0,0},{1,32},{2,64},{3,96},{4,128},{5,160},{6,192},{7,224},{32,1},... | collective-permute-start | bytes 393224 | tf_op jit(solution)/shard_map/ppermute | solution.py:208
  159.8 38.5 %copy-start = (bf16[512,3072]{1,0:T(8,128)(2,1)S(1)}, bf16[512,3072]{1,0:T(8,128)(2,1)}, u32[]{:S(2)}) copy-start(bf16[512,3072]{1,0:T(8,128)(2,1)} %param.16) | copy-start | bytes 9437188
  202.2 15.1 %all-to-all-start.6 = ((bf16[8,32,1024]{2,1,0:T(8,128)(2,1)}), bf16[8,32,1024]{2,1,0:T(8,128)(2,1)S(1)}, u32[]{:S(2)}, u32[]{:S(2)}) async-start(bf16[8,32,1024]{2,1,0:T(8,128)(2,1)} %bitcast.25), calls=%async_computation.6 | async-start | bytes 1048576 | tf_op jit(solution)/shard_map/all_to_all | solution.py:30
  210.8 22.3 %copy-start.3 = (f32[1024]{0:T(1024)}, f32[1024]{0:T(1024)S(1)}, u32[]{:S(2)}) copy-start(f32[1024]{0:T(1024)S(1)} %fusion.72) | copy-start | bytes 12292
  230.5 42.7 %copy-start.1 = (bf16[512,3072]{1,0:T(8,128)(2,1)S(1)}, bf16[512,3072]{1,0:T(8,128)(2,1)}, u32[]{:S(2)}) copy-start(bf16[512,3072]{1,0:T(8,128)(2,1)} %param.16) | copy-start | bytes 9437188
  233.1 20.7 %all-to-all-start.8 = ((bf16[8,32,1024]{2,1,0:T(8,128)(2,1)}), bf16[8,32,1024]{2,1,0:T(8,128)(2,1)}, u32[]{:S(2)}, u32[]{:S(2)}) async-start(bf16[8,32,1024]{2,1,0:T(8,128)(2,1)} %bitcast.127), calls=%async_computation.8 | async-start | bytes 1048576 | tf_op jit(solution)/shard_map/all_to_all | solution.py:30
  276.3 13.6 %all-to-all-start.10 = ((bf16[16,16,1024]{2,1,0:T(8,128)(2,1)}), bf16[16,16,1024]{2,1,0:T(8,128)(2,1)}, u32[]{:S(2)}, u32[]{:S(2)}) async-start(bf16[16,16,1024]{2,1,0:T(8,128)(2,1)} %bitcast.118), calls=%async_computation.10 | async-start | bytes 1048576 | tf_op jit(solution)/shard_map/all_to_all | solution.py:30
  308.5 14.5 %all-to-all-start.12 = ((bf16[8,32,512]{2,1,0:T(8,128)(2,1)}), bf16[8,32,512]{2,1,0:T(8,128)(2,1)}, u32[]{:S(2)}, u32[]{:S(2)}) async-start(bf16[8,32,512]{2,1,0:T(8,128)(2,1)} %bitcast.141), calls=%async_computation.12 | async-start | bytes 524288 | tf_op jit(solution)/shard_map/all_to_all | solution.py:30
  324.7 29.1 %copy-start.5 = (f32[1024]{0:T(1024)S(1)}, f32[1024]{0:T(1024)}, u32[]{:S(2)}) copy-start(f32[1024]{0:T(1024)} %fusion.73) | copy-start | bytes 12292
  404.7 15.3 %copy-start.4 = (f32[1024]{0:T(1024)S(1)}, f32[1024]{0:T(1024)}, u32[]{:S(2)}) copy-start(f32[1024]{0:T(1024)} %copy-done.3) | copy-start | bytes 12292
  462.1 4.9 copy-start.2
  463.4 21.1 %all-to-all-start.21 = ((bf16[8,32,2048]{2,1,0:T(8,128)(2,1)}), bf16[8,32,2048]{2,1,0:T(8,128)(2,1)S(1)}, u32[]{:S(2)}, u32[]{:S(2)}) async-start(bf16[8,32,2048]{2,1,0:T(8,128)(2,1)} %broadcast_in_dim.35), calls=%async_computation.21 | async-start | bytes 2097152 | tf_op jit(solution)/shard_map/all_to_all | solution.py:30
  467.0 27.9 %collective-permute-start.11 = (f32[16,512]{1,0:T(8,128)S(1)}, f32[16,512]{1,0:T(8,128)S(1)}, u32[]{:S(2)}, u32[]{:S(2)}) collective-permute-start(f32[16,512]{1,0:T(8,128)S(1)} %get-tuple-element.41), channel_id=1, source_target_pairs={{0,0},{1,32},{2,64},{3,96},{4,128},{5,160},{6,192},{7,224},{8,1},{... | collective-permute-start | bytes 98312 | tf_op jit(solution)/shard_map/ppermute | solution.py:244
  475.6 19.3 %collective-permute-start.12 = (f32[16,512]{1,0:T(8,128)S(1)}, f32[16,512]{1,0:T(8,128)S(1)}, u32[]{:S(2)}, u32[]{:S(2)}) collective-permute-start(f32[16,512]{1,0:T(8,128)S(1)} %get-tuple-element.42), channel_id=1, source_target_pairs={{0,1},{1,33},{2,65},{3,97},{4,129},{5,161},{6,193},{7,225},{8,0},{... | collective-permute-start | bytes 98312 | tf_op jit(solution)/shard_map/ppermute | solution.py:244
  490.0 13.0 %all-to-all-start.22 = ((bf16[4,64,1024]{2,1,0:T(8,128)(2,1)}), bf16[4,64,1024]{2,1,0:T(8,128)(2,1)S(1)}, u32[]{:S(2)}, u32[]{:S(2)}) async-start(bf16[4,64,1024]{2,1,0:T(8,128)(2,1)} %bitcast.50), calls=%async_computation.22 | async-start | bytes 1048576 | tf_op jit(solution)/shard_map/all_to_all | solution.py:30
  503.2 15.2 %collective-permute-start.8 = (f32[32,1024]{1,0:T(8,128)S(1)}, f32[32,1024]{1,0:T(8,128)S(1)}, u32[]{:S(2)}, u32[]{:S(2)}) collective-permute-start(f32[32,1024]{1,0:T(8,128)S(1)} %get-tuple-element.27), channel_id=1, source_target_pairs={{0,0},{1,64},{2,128},{3,192},{32,32},{33,96},{34,160},{35,224},{64... | collective-permute-start | bytes 393224 | tf_op jit(solution)/shard_map/ppermute | solution.py:266
  503.9 14.5 %collective-permute-start.9 = (f32[32,1024]{1,0:T(8,128)S(1)}, f32[32,1024]{1,0:T(8,128)S(1)}, u32[]{:S(2)}, u32[]{:S(2)}) collective-permute-start(f32[32,1024]{1,0:T(8,128)S(1)} %get-tuple-element.28), channel_id=1, source_target_pairs={{0,32},{1,96},{2,160},{3,224},{32,0},{33,64},{34,128},{35,192},{64... | collective-permute-start | bytes 393224 | tf_op jit(solution)/shard_map/ppermute | solution.py:266
  505.1 17.2 %collective-permute-start.10 = (f32[32,1024]{1,0:T(8,128)S(1)}, f32[32,1024]{1,0:T(8,128)S(1)}, u32[]{:S(2)}, u32[]{:S(2)}) collective-permute-start(f32[32,1024]{1,0:T(8,128)S(1)} %maximum_select_fusion.3), channel_id=1, source_target_pairs={{0,0},{1,32},{2,64},{3,96},{4,128},{5,160},{6,192},{7,224},{32,1},... | collective-permute-start | bytes 393224 | tf_op jit(solution)/shard_map/ppermute | solution.py:251

commit v4 on v3

--- a/solution.py
+++ b/solution.py
@@ -185,8 +185,8 @@
         return value.reshape(2, 8, 16, 1024).transpose(1, 0, 2, 3).reshape(256, 1024)
 
     halves = form_loads(elem_mat, elem_deriv, elem_disp, elem_sens, design_var, dof_rows)
-    halves = exchange(halves, C).astype(F32)
-    half = (halves[0] + halves[1]).astype(BF)
+    halves = exchange(halves, C)
+    half = halves[0] + halves[1]
     top = exchange(half[:, :, :2048].reshape(4, 64, 2048), X)
 
     def halved(value, bit):

time: 531 us -> 529 us (level)
  no operation moved by 1% of the time
where the time goes in v4:
time: 529 us; the launch traced here: 522 us
  blocking collectives  205 us (39%)
  waiting for transfers between devices  126 us (24%)
  starting transfers between devices  106 us (20%)
  matrix products  34.4 us (7%)
  other arithmetic  23.7 us (4%)
  Pallas kernels  17.4 us (3%)
  local copies, waits for them, and re-layouts  7.7 us (1%)
    all_to_all x12, blocking collectives, exchange(): return lax.all_to_all(chunks, axes, split_axis=0, concat_axis=0, tiled=True)  205 us
    all_to_all x11, waiting for transfers between devices, exchange(): return lax.all_to_all(chunks, axes, split_axis=0, concat_axis=0, tiled=True)  74.9 us
    all_to_all x11, starting transfers between devices, exchange(): return lax.all_to_all(chunks, axes, split_axis=0, concat_axis=0, tiled=True)  54.8 us
    ppermute x3, waiting for transfers between devices, halved(): return kept.astype(F32) + lax.ppermute(sent, Z, perm).astype(F32)  33.3 us
    ppermute x4, starting transfers between devices, body(): got.append(lax.ppermute(sent, (Z, H, L, X), perm))  20.9 us
    dot_general x10, matrix products, dot_t(): lax.dot_general(a, b, (((1,), (1,)), ((), ())), preferred_element_type=F32)  18.7 us
    pallas_call x1, Pallas kernels, form_loads(): pl.pallas_call(loads_kernel, grid=(128 // E_STEP,), in_specs=[smem, smem,...  17.4 us
    dot_general x10, matrix products, dot(): lax.dot_general(a, b, (((1,), (0,)), ((), ())), preferred_element_type=F32)  15.7 us
  transfers between devices with their start and end apart: 24, of which 15 were waited for; matrix products, arithmetic and copies ran while one was open for 4% of the time, Pallas kernels for 0%

profile of v4, /device:TPU:8, one launch (start us, length us, event | category | flops | bytes accessed | tf_op | source)
XLA Modules:
  0.0 521.6 jit_solution(2766183328694998528)
XLA Ops:
  7.7 17.4 %loads.1 = bf16[2,8,32,3584]{3,2,1,0:T(8,128)(2,1)} custom-call(s32[128]{0:T(128)} %fusion.75.block_ref, s32[128]{0:T(128)} %var_ref.1, s32[128,1,24]{2,1,0:T(1,128)} %bitcast.146, bf16[128,24,32]{2,1,0:T(8,128)(2,1)} %maximum_bitcast_fusion.table_ref, bf16[128,24,512]{2,1,0:T(8,128)(2,1)} %sens_ref.1), custom_call_target="tpu_custom_call" | custom-call | flops 800000000 | bytes 8000000 | tf_op jit(solution)/shard_map/loads/pallas_call | solution.py:109
  25.1 5.4 %all-to-all-start = ((bf16[2,8,32,3584]{3,2,1,0:T(8,128)(2,1)}), bf16[2,8,32,3584]{3,2,1,0:T(8,128)(2,1)}, u32[]{:S(2)}, u32[]{:S(2)}) async-start(bf16[2,8,32,3584]{3,2,1,0:T(8,128)(2,1)} %loads.1), calls=%async_computation | async-start | bytes 7340032 | tf_op jit(solution)/shard_map/all_to_all | solution.py:30
  48.6 10.9 %all-to-all-done.1 = bf16[4,64,2048]{2,1,0:T(8,128)(2,1)S(1)} async-done(((bf16[4,64,2048]{2,1,0:T(8,128)(2,1)}), bf16[4,64,2048]{2,1,0:T(8,128)(2,1)S(1)}, u32[]{:S(2)}, u32[]{:S(2)}) %all-to-all-start.1) | async-done | bytes 1048608 | tf_op jit(solution)/shard_map/all_to_all | solution.py:30
  60.7 7.6 %all-to-all-start.2 = ((bf16[8,64,1024]{2,1,0:T(8,128)(2,1)}), bf16[8,64,1024]{2,1,0:T(8,128)(2,1)S(1)}, u32[]{:S(2)}, u32[]{:S(2)}) async-start(bf16[8,64,1024]{2,1,0:T(8,128)(2,1)} %bitcast.10), calls=%async_computation.2 | async-start | bytes 2097152 | tf_op jit(solution)/shard_map/all_to_all | solution.py:30
  72.6 28.7 %collective-permute-done.1 = bf16[2,32,1536]{2,1,0:T(8,128)(2,1)S(1)} collective-permute-done((bf16[2,32,1536]{2,1,0:T(8,128)(2,1)S(1)}, bf16[2,32,1536]{2,1,0:T(8,128)(2,1)S(1)}, u32[]{:S(2)}, u32[]{:S(2)}) %collective-permute-start.1) | collective-permute-done | bytes 196640 | tf_op jit(solution)/shard_map/ppermute | solution.py:198
  110.3 7.5 %all-to-all-done.3 = bf16[4,64,1024]{2,1,0:T(8,128)(2,1)S(1)} async-done(((bf16[4,64,1024]{2,1,0:T(8,128)(2,1)}), bf16[4,64,1024]{2,1,0:T(8,128)(2,1)S(1)}, u32[]{:S(2)}, u32[]{:S(2)}) %all-to-all-start.3) | async-done | bytes 524320 | tf_op jit(solution)/shard_map/all_to_all | solution.py:30
  127.4 4.7 collective-permute-start.5
  137.3 6.7 %collective-permute-start.4 = (f32[32,1024]{1,0:T(8,128)S(1)}, f32[32,1024]{1,0:T(8,128)S(1)}, u32[]{:S(2)}, u32[]{:S(2)}) collective-permute-start(f32[32,1024]{1,0:T(8,128)S(1)} %slice.189), channel_id=1, source_target_pairs={{0,0},{1,32},{2,64},{3,96},{4,128},{5,160},{6,192},{7,224},{32,1},... | collective-permute-start | bytes 393224 | tf_op jit(solution)/shard_map/ppermute | solution.py:208
  144.0 12.0 %collective-permute-done.5 = f32[16,512]{1,0:T(8,128)S(1)} collective-permute-done((f32[16,512]{1,0:T(8,128)S(1)}, f32[16,512]{1,0:T(8,128)S(1)}, u32[]{:S(2)}, u32[]{:S(2)}) %collective-permute-start.5) | collective-permute-done | bytes 32800 | tf_op jit(solution)/shard_map/ppermute | solution.py:219
  158.9 38.2 %all_to_all.115 = bf16[8,32,2048]{2,1,0:T(8,128)(2,1)S(1)} all-to-all(bf16[8,32,2048]{2,1,0:T(8,128)(2,1)S(1)} %broadcast_in_dim.27), channel_id=1, replica_groups=mesh['z'=8,'c'=2,'h'=2,'l'=2,'x'=4] {'z'}, dimensions={0} | all-to-all | bytes 2097152 | tf_op jit(solution)/shard_map/all_to_all | solution.py:30
  201.0 7.9 %all-to-all-start.6 = ((bf16[8,32,1024]{2,1,0:T(8,128)(2,1)}), bf16[8,32,1024]{2,1,0:T(8,128)(2,1)S(1)}, u32[]{:S(2)}, u32[]{:S(2)}) async-start(bf16[8,32,1024]{2,1,0:T(8,128)(2,1)} %bitcast.25), calls=%async_computation.6 | async-start | bytes 1048576 | tf_op jit(solution)/shard_map/all_to_all | solution.py:30
  209.6 6.6 %all-to-all-done.6 = bf16[8,32,1024]{2,1,0:T(8,128)(2,1)S(1)} async-done(((bf16[8,32,1024]{2,1,0:T(8,128)(2,1)}), bf16[8,32,1024]{2,1,0:T(8,128)(2,1)S(1)}, u32[]{:S(2)}, u32[]{:S(2)}) %all-to-all-start.6) | async-done | bytes 524320 | tf_op jit(solution)/shard_map/all_to_all | solution.py:30
  216.3 11.2 %all_to_all.116 = bf16[8,32,1024]{2,1,0:T(8,128)(2,1)S(1)} all-to-all(bf16[8,32,1024]{2,1,0:T(8,128)(2,1)S(1)} %broadcast_in_dim.28), channel_id=1, replica_groups=mesh['z'=8,'c'=2,'h'=2,'l'=2,'x'=4] {'l','x'}, dimensions={0} | all-to-all | bytes 1048576 | tf_op jit(solution)/shard_map/all_to_all | solution.py:30
  236.7 15.6 %all-to-all-done.8 = bf16[8,32,1024]{2,1,0:T(8,128)(2,1)} async-done(((bf16[8,32,1024]{2,1,0:T(8,128)(2,1)}), bf16[8,32,1024]{2,1,0:T(8,128)(2,1)}, u32[]{:S(2)}, u32[]{:S(2)}) %all-to-all-start.8) | async-done | bytes 524320 | tf_op jit(solution)/shard_map/all_to_all | solution.py:30
  253.5 18.2 %all_to_all.117 = bf16[8,32,1024]{2,1,0:T(8,128)(2,1)S(1)} all-to-all(bf16[8,32,1024]{2,1,0:T(8,128)(2,1)S(1)} %broadcast_in_dim.29), channel_id=1, replica_groups=mesh['z'=8,'c'=2,'h'=2,'l'=2,'x'=4] {'z'}, dimensions={0} | all-to-all | bytes 1048576 | tf_op jit(solution)/shard_map/all_to_all | solution.py:30
  274.8 5.5 %all-to-all-start.10 = ((bf16[16,16,1024]{2,1,0:T(8,128)(2,1)}), bf16[16,16,1024]{2,1,0:T(8,128)(2,1)}, u32[]{:S(2)}, u32[]{:S(2)}) async-start(bf16[16,16,1024]{2,1,0:T(8,128)(2,1)} %bitcast.118), calls=%async_computation.10 | async-start | bytes 1048576 | tf_op jit(solution)/shard_map/all_to_all | solution.py:30
  281.4 7.0 %all-to-all-done.10 = bf16[16,16,1024]{2,1,0:T(8,128)(2,1)} async-done(((bf16[16,16,1024]{2,1,0:T(8,128)(2,1)}), bf16[16,16,1024]{2,1,0:T(8,128)(2,1)}, u32[]{:S(2)}, u32[]{:S(2)}) %all-to-all-start.10) | async-done | bytes 524320 | tf_op jit(solution)/shard_map/all_to_all | solution.py:30
  290.4 13.1 %all_to_all.118 = bf16[16,16,1024]{2,1,0:T(8,128)(2,1)S(1)} all-to-all(bf16[16,16,1024]{2,1,0:T(8,128)(2,1)S(1)} %broadcast_in_dim.30), channel_id=1, replica_groups=mesh['z'=8,'c'=2,'h'=2,'l'=2,'x'=4] {'h','l','x'}, dimensions={0} | all-to-all | bytes 1048576 | tf_op jit(solution)/shard_map/all_to_all | solution.py:30
  312.2 9.3 %all-to-all-done.12 = bf16[8,32,512]{2,1,0:T(8,128)(2,1)} async-done(((bf16[8,32,512]{2,1,0:T(8,128)(2,1)}), bf16[8,32,512]{2,1,0:T(8,128)(2,1)}, u32[]{:S(2)}, u32[]{:S(2)}) %all-to-all-start.12) | async-done | bytes 262176 | tf_op jit(solution)/shard_map/all_to_all | solution.py:30
  323.3 12.9 %all_to_all.119 = bf16[8,32,512]{2,1,0:T(8,128)(2,1)S(1)} all-to-all(bf16[8,32,512]{2,1,0:T(8,128)(2,1)S(1)} %broadcast_in_dim.31), channel_id=1, replica_groups=mesh['z'=8,'c'=2,'h'=2,'l'=2,'x'=4] {'z'}, dimensions={0} | all-to-all | bytes 524288 | tf_op jit(solution)/shard_map/all_to_all | solution.py:30
  339.0 13.3 %all_to_all.120 = bf16[16,16,1024]{2,1,0:T(8,128)(2,1)S(1)} all-to-all(bf16[16,16,1024]{2,1,0:T(8,128)(2,1)S(1)} %bitcast.125), channel_id=1, replica_groups=mesh['z'=8,'c'=2,'h'=2,'l'=2,'x'=4] {'h','l','x'}, dimensions={0} | all-to-all | bytes 1048576 | tf_op jit(solution)/shard_map/all_to_all | solution.py:30
  353.0 12.9 %all_to_all.121 = bf16[16,16,1024]{2,1,0:T(8,128)(2,1)S(1)} all-to-all(bf16[16,16,1024]{2,1,0:T(8,128)(2,1)S(1)} %broadcast_in_dim.32), channel_id=1, replica_groups=mesh['z'=8,'c'=2,'h'=2,'l'=2,'x'=4] {'h','l','x'}, dimensions={0} | all-to-all | bytes 1048576 | tf_op jit(solution)/shard_map/all_to_all | solution.py:30
  368.1 17.8 %all_to_all.122 = bf16[8,32,1024]{2,1,0:T(8,128)(2,1)S(1)} all-to-all(bf16[8,32,1024]{2,1,0:T(8,128)(2,1)S(1)} %bitcast.132), channel_id=1, replica_groups=mesh['z'=8,'c'=2,'h'=2,'l'=2,'x'=4] {'z'}, dimensions={0} | all-to-all | bytes 1048576 | tf_op jit(solution)/shard_map/all_to_all | solution.py:30
  386.1 17.1 %all_to_all.123 = bf16[8,32,1024]{2,1,0:T(8,128)(2,1)S(1)} all-to-all(bf16[8,32,1024]{2,1,0:T(8,128)(2,1)S(1)} %broadcast_in_dim.33), channel_id=1, replica_groups=mesh['z'=8,'c'=2,'h'=2,'l'=2,'x'=4] {'z'}, dimensions={0} | all-to-all | bytes 1048576 | tf_op jit(solution)/shard_map/all_to_all | solution.py:30
  406.6 11.9 %all_to_all.124 = bf16[8,32,1024]{2,1,0:T(8,128)(2,1)S(1)} all-to-all(bf16[8,32,1024]{2,1,0:T(8,128)(2,1)S(1)} %bitcast.123), channel_id=1, replica_groups=mesh['z'=8,'c'=2,'h'=2,'l'=2,'x'=4] {'l','x'}, dimensions={0} | all-to-all | bytes 1048576 | tf_op jit(solution)/shard_map/all_to_all | solution.py:30
  418.6 11.2 %all_to_all.125 = bf16[8,32,1024]{2,1,0:T(8,128)(2,1)S(1)} all-to-all(bf16[8,32,1024]{2,1,0:T(8,128)(2,1)S(1)} %broadcast_in_dim.34), channel_id=1, replica_groups=mesh['z'=8,'c'=2,'h'=2,'l'=2,'x'=4] {'l','x'}, dimensions={0} | all-to-all | bytes 1048576 | tf_op jit(solution)/shard_map/all_to_all | solution.py:30
  432.9 27.6 %all_to_all.126 = bf16[8,32,2048]{2,1,0:T(8,128)(2,1)S(1)} all-to-all(bf16[8,32,2048]{2,1,0:T(8,128)(2,1)S(1)} %bitcast.117), channel_id=1, replica_groups=mesh['z'=8,'c'=2,'h'=2,'l'=2,'x'=4] {'z'}, dimensions={0} | all-to-all | bytes 2097152 | tf_op jit(solution)/shard_map/all_to_all | solution.py:30
  465.5 8.6 %collective-permute-start.11 = (f32[16,512]{1,0:T(8,128)S(1)}, f32[16,512]{1,0:T(8,128)S(1)}, u32[]{:S(2)}, u32[]{:S(2)}) collective-permute-start(f32[16,512]{1,0:T(8,128)S(1)} %get-tuple-element.41), channel_id=1, source_target_pairs={{0,0},{1,32},{2,64},{3,96},{4,128},{5,160},{6,192},{7,224},{8,1},{... | collective-permute-start | bytes 98312 | tf_op jit(solution)/shard_map/ppermute | solution.py:244
  477.2 5.8 %all-to-all-done.21 = bf16[8,32,2048]{2,1,0:T(8,128)(2,1)S(1)} async-done(((bf16[8,32,2048]{2,1,0:T(8,128)(2,1)}), bf16[8,32,2048]{2,1,0:T(8,128)(2,1)S(1)}, u32[]{:S(2)}, u32[]{:S(2)}) %all-to-all-start.21) | async-done | bytes 1048608 | tf_op jit(solution)/shard_map/all_to_all | solution.py:30
  488.5 4.9 all-to-all-start.22
  493.4 8.0 %all-to-all-done.22 = bf16[4,64,1024]{2,1,0:T(8,128)(2,1)S(1)} async-done(((bf16[4,64,1024]{2,1,0:T(8,128)(2,1)}), bf16[4,64,1024]{2,1,0:T(8,128)(2,1)S(1)}, u32[]{:S(2)}, u32[]{:S(2)}) %all-to-all-start.22) | async-done | bytes 524320 | tf_op jit(solution)/shard_map/all_to_all | solution.py:30
  503.6 13.3 %collective-permute-start.10 = (f32[32,1024]{1,0:T(8,128)S(1)}, f32[32,1024]{1,0:T(8,128)S(1)}, u32[]{:S(2)}, u32[]{:S(2)}) collective-permute-start(f32[32,1024]{1,0:T(8,128)S(1)} %maximum_select_fusion.3), channel_id=1, source_target_pairs={{0,0},{1,32},{2,64},{3,96},{4,128},{5,160},{6,192},{7,224},{32,1},... | collective-permute-start | bytes 393224 | tf_op jit(solution)/shard_map/ppermute | solution.py:251
  (152 shorter events, 121.9 us)
Async XLA Ops:
  25.1 9.5 %all-to-all-start = ((bf16[2,8,32,3584]{3,2,1,0:T(8,128)(2,1)}), bf16[2,8,32,3584]{3,2,1,0:T(8,128)(2,1)}, u32[]{:S(2)}, u32[]{:S(2)}) async-start(bf16[2,8,32,3584]{3,2,1,0:T(8,128)(2,1)} %loads.1), calls=%async_computation | async-start | bytes 7340032 | tf_op jit(solution)/shard_map/all_to_all | solution.py:30
  37.0 11.5 %collective-permute-start = (bf16[4,32,1536]{2,1,0:T(8,128)(2,1)S(1)}, bf16[4,32,1536]{2,1,0:T(8,128)(2,1)S(1)}, u32[]{:S(2)}, u32[]{:S(2)}) collective-permute-start(bf16[4,32,1536]{2,1,0:T(8,128)(2,1)S(1)} %select_bitcast_fusion), channel_id=1, source_target_pairs={{0,32},{32,0},{64,96},{96,64},{128,160},{160,128},{192,224},{224,1... | collective-permute-start | bytes 1179656 | tf_op jit(solution)/shard_map/ppermute | solution.py:198
  40.1 19.4 %all-to-all-start.1 = ((bf16[4,64,2048]{2,1,0:T(8,128)(2,1)}), bf16[4,64,2048]{2,1,0:T(8,128)(2,1)S(1)}, u32[]{:S(2)}, u32[]{:S(2)}) async-start(bf16[4,64,2048]{2,1,0:T(8,128)(2,1)} %bitcast.116), calls=%async_computation.1 | async-start | bytes 2097152 | tf_op jit(solution)/shard_map/all_to_all | solution.py:30
  44.4 75.7 %collective-permute-start.3 = (bf16[3584,512]{1,0:T(8,128)(2,1)}, bf16[3584,512]{1,0:T(8,128)(2,1)}, u32[]{:S(2)}, u32[]{:S(2)}) collective-permute-start(bf16[3584,512]{1,0:T(8,128)(2,1)} %param.15), channel_id=1, source_target_pairs={{0,16},{16,0},{1,17},{17,1},{2,18},{18,2},{3,19},{19,3},{4,20},{20... | collective-permute-start | bytes 11010056 | tf_op jit(solution)/shard_map/ppermute | solution.py:146
  48.6 22.7 %copy-start.6 = (s32[7]{0:T(128)S(1)}, s32[7]{0:T(128)}, u32[]{:S(2)}) copy-start(s32[7]{0:T(128)} %param.17) | copy-start | bytes 88
  60.7 44.4 %all-to-all-start.2 = ((bf16[8,64,1024]{2,1,0:T(8,128)(2,1)}), bf16[8,64,1024]{2,1,0:T(8,128)(2,1)S(1)}, u32[]{:S(2)}, u32[]{:S(2)}) async-start(bf16[8,64,1024]{2,1,0:T(8,128)(2,1)} %bitcast.10), calls=%async_computation.2 | async-start | bytes 2097152 | tf_op jit(solution)/shard_map/all_to_all | solution.py:30
  68.3 33.0 %collective-permute-start.1 = (bf16[2,32,1536]{2,1,0:T(8,128)(2,1)S(1)}, bf16[2,32,1536]{2,1,0:T(8,128)(2,1)S(1)}, u32[]{:S(2)}, u32[]{:S(2)}) collective-permute-start(bf16[2,32,1536]{2,1,0:T(8,128)(2,1)S(1)} %fusion.62), channel_id=1, source_target_pairs={{0,64},{32,96},{64,0},{96,32},{128,192},{160,224},{192,128},{224,1... | collective-permute-start | bytes 589832 | tf_op jit(solution)/shard_map/ppermute | solution.py:198
  101.4 8.9 %collective-permute-start.2 = (bf16[1,32,1536]{2,1,0:T(8,128)(2,1)S(1)}, bf16[1,32,1536]{2,1,0:T(8,128)(2,1)S(1)}, u32[]{:S(2)}, u32[]{:S(2)}) collective-permute-start(bf16[1,32,1536]{2,1,0:T(8,128)(2,1)S(1)} %fusion.64), channel_id=1, source_target_pairs={{0,128},{32,160},{64,192},{96,224},{128,0},{160,32},{192,64},{224,... | collective-permute-start | bytes 294920 | tf_op jit(solution)/shard_map/ppermute | solution.py:198
  106.2 11.5 %all-to-all-start.3 = ((bf16[4,64,1024]{2,1,0:T(8,128)(2,1)}), bf16[4,64,1024]{2,1,0:T(8,128)(2,1)S(1)}, u32[]{:S(2)}, u32[]{:S(2)}) async-start(bf16[4,64,1024]{2,1,0:T(8,128)(2,1)} %broadcast_in_dim.26), calls=%async_computation.3 | async-start | bytes 1048576 | tf_op jit(solution)/shard_map/all_to_all | solution.py:30
  123.4 35.1 %all-to-all-start.4 = ((bf16[8,32,2048]{2,1,0:T(8,128)(2,1)}), bf16[8,32,2048]{2,1,0:T(8,128)(2,1)S(1)}, u32[]{:S(2)}, u32[]{:S(2)}) async-start(bf16[8,32,2048]{2,1,0:T(8,128)(2,1)} %bitcast.22), calls=%async_computation.4 | async-start | bytes 2097152 | tf_op jit(solution)/shard_map/all_to_all | solution.py:30
  127.4 70.4 %collective-permute-start.7 = (bf16[512,3072]{1,0:T(8,128)(2,1)}, bf16[512,3072]{1,0:T(8,128)(2,1)}, u32[]{:S(2)}, u32[]{:S(2)}) collective-permute-start(bf16[512,3072]{1,0:T(8,128)(2,1)} %param.16), channel_id=1, source_target_pairs={{0,16},{16,0},{1,17},{17,1},{2,18},{18,2},{3,19},{19,3},{4,20},{20... | collective-permute-start | bytes 9437192 | tf_op jit(solution)/shard_map/ppermute | solution.py:147
  127.4 28.6 %collective-permute-start.5 = (f32[16,512]{1,0:T(8,128)S(1)}, f32[16,512]{1,0:T(8,128)S(1)}, u32[]{:S(2)}, u32[]{:S(2)}) collective-permute-start(f32[16,512]{1,0:T(8,128)S(1)} %get-tuple-element.33), channel_id=1, source_target_pairs={{0,0},{1,8},{2,32},{3,40},{4,64},{5,72},{6,96},{7,104},{8,128},{9,... | collective-permute-start | bytes 98312 | tf_op jit(solution)/shard_map/ppermute | solution.py:219
  132.1 23.9 %collective-permute-start.6 = (f32[16,512]{1,0:T(8,128)S(1)}, f32[16,512]{1,0:T(8,128)S(1)}, u32[]{:S(2)}, u32[]{:S(2)}) collective-permute-start(f32[16,512]{1,0:T(8,128)S(1)} %get-tuple-element.34), channel_id=1, source_target_pairs={{0,8},{1,0},{2,40},{3,32},{4,72},{5,64},{6,104},{7,96},{8,136},{9,... | collective-permute-start | bytes 98312 | tf_op jit(solution)/shard_map/ppermute | solution.py:219
  137.3 21.2 %collective-permute-start.4 = (f32[32,1024]{1,0:T(8,128)S(1)}, f32[32,1024]{1,0:T(8,128)S(1)}, u32[]{:S(2)}, u32[]{:S(2)}) collective-permute-start(f32[32,1024]{1,0:T(8,128)S(1)} %slice.189), channel_id=1, source_target_pairs={{0,0},{1,32},{2,64},{3,96},{4,128},{5,160},{6,192},{7,224},{32,1},... | collective-permute-start | bytes 393224 | tf_op jit(solution)/shard_map/ppermute | solution.py:208
  158.5 38.5 %copy-start = (bf16[512,3072]{1,0:T(8,128)(2,1)S(1)}, bf16[512,3072]{1,0:T(8,128)(2,1)}, u32[]{:S(2)}) copy-start(bf16[512,3072]{1,0:T(8,128)(2,1)} %param.16) | copy-start | bytes 9437188
  201.0 15.1 %all-to-all-start.6 = ((bf16[8,32,1024]{2,1,0:T(8,128)(2,1)}), bf16[8,32,1024]{2,1,0:T(8,128)(2,1)S(1)}, u32[]{:S(2)}, u32[]{:S(2)}) async-start(bf16[8,32,1024]{2,1,0:T(8,128)(2,1)} %bitcast.25), calls=%async_computation.6 | async-start | bytes 1048576 | tf_op jit(solution)/shard_map/all_to_all | solution.py:30
  209.6 22.3 %copy-start.3 = (f32[1024]{0:T(1024)}, f32[1024]{0:T(1024)S(1)}, u32[]{:S(2)}) copy-start(f32[1024]{0:T(1024)S(1)} %fusion.71) | copy-start | bytes 12292
  229.2 42.4 %copy-start.1 = (bf16[512,3072]{1,0:T(8,128)(2,1)S(1)}, bf16[512,3072]{1,0:T(8,128)(2,1)}, u32[]{:S(2)}) copy-start(bf16[512,3072]{1,0:T(8,128)(2,1)} %param.16) | copy-start | bytes 9437188
  231.9 20.4 %all-to-all-start.8 = ((bf16[8,32,1024]{2,1,0:T(8,128)(2,1)}), bf16[8,32,1024]{2,1,0:T(8,128)(2,1)}, u32[]{:S(2)}, u32[]{:S(2)}) async-start(bf16[8,32,1024]{2,1,0:T(8,128)(2,1)} %bitcast.127), calls=%async_computation.8 | async-start | bytes 1048576 | tf_op jit(solution)/shard_map/all_to_all | solution.py:30
  274.8 13.6 %all-to-all-start.10 = ((bf16[16,16,1024]{2,1,0:T(8,128)(2,1)}), bf16[16,16,1024]{2,1,0:T(8,128)(2,1)}, u32[]{:S(2)}, u32[]{:S(2)}) async-start(bf16[16,16,1024]{2,1,0:T(8,128)(2,1)} %bitcast.118), calls=%async_computation.10 | async-start | bytes 1048576 | tf_op jit(solution)/shard_map/all_to_all | solution.py:30
  307.0 14.5 %all-to-all-start.12 = ((bf16[8,32,512]{2,1,0:T(8,128)(2,1)}), bf16[8,32,512]{2,1,0:T(8,128)(2,1)}, u32[]{:S(2)}, u32[]{:S(2)}) async-start(bf16[8,32,512]{2,1,0:T(8,128)(2,1)} %bitcast.141), calls=%async_computation.12 | async-start | bytes 524288 | tf_op jit(solution)/shard_map/all_to_all | solution.py:30
  323.3 29.1 %copy-start.5 = (f32[1024]{0:T(1024)S(1)}, f32[1024]{0:T(1024)}, u32[]{:S(2)}) copy-start(f32[1024]{0:T(1024)} %fusion.72) | copy-start | bytes 12292
  403.2 15.3 %copy-start.4 = (f32[1024]{0:T(1024)S(1)}, f32[1024]{0:T(1024)}, u32[]{:S(2)}) copy-start(f32[1024]{0:T(1024)} %copy-done.3) | copy-start | bytes 12292
  460.6 4.9 copy-start.2
  461.9 21.1 %all-to-all-start.21 = ((bf16[8,32,2048]{2,1,0:T(8,128)(2,1)}), bf16[8,32,2048]{2,1,0:T(8,128)(2,1)S(1)}, u32[]{:S(2)}, u32[]{:S(2)}) async-start(bf16[8,32,2048]{2,1,0:T(8,128)(2,1)} %broadcast_in_dim.35), calls=%async_computation.21 | async-start | bytes 2097152 | tf_op jit(solution)/shard_map/all_to_all | solution.py:30
  465.5 27.9 %collective-permute-start.11 = (f32[16,512]{1,0:T(8,128)S(1)}, f32[16,512]{1,0:T(8,128)S(1)}, u32[]{:S(2)}, u32[]{:S(2)}) collective-permute-start(f32[16,512]{1,0:T(8,128)S(1)} %get-tuple-element.41), channel_id=1, source_target_pairs={{0,0},{1,32},{2,64},{3,96},{4,128},{5,160},{6,192},{7,224},{8,1},{... | collective-permute-start | bytes 98312 | tf_op jit(solution)/shard_map/ppermute | solution.py:244
  474.1 19.3 %collective-permute-start.12 = (f32[16,512]{1,0:T(8,128)S(1)}, f32[16,512]{1,0:T(8,128)S(1)}, u32[]{:S(2)}, u32[]{:S(2)}) collective-permute-start(f32[16,512]{1,0:T(8,128)S(1)} %get-tuple-element.42), channel_id=1, source_target_pairs={{0,1},{1,33},{2,65},{3,97},{4,129},{5,161},{6,193},{7,225},{8,0},{... | collective-permute-start | bytes 98312 | tf_op jit(solution)/shard_map/ppermute | solution.py:244
  488.5 13.0 %all-to-all-start.22 = ((bf16[4,64,1024]{2,1,0:T(8,128)(2,1)}), bf16[4,64,1024]{2,1,0:T(8,128)(2,1)S(1)}, u32[]{:S(2)}, u32[]{:S(2)}) async-start(bf16[4,64,1024]{2,1,0:T(8,128)(2,1)} %bitcast.50), calls=%async_computation.22 | async-start | bytes 1048576 | tf_op jit(solution)/shard_map/all_to_all | solution.py:30
  501.7 15.2 %collective-permute-start.8 = (f32[32,1024]{1,0:T(8,128)S(1)}, f32[32,1024]{1,0:T(8,128)S(1)}, u32[]{:S(2)}, u32[]{:S(2)}) collective-permute-start(f32[32,1024]{1,0:T(8,128)S(1)} %get-tuple-element.27), channel_id=1, source_target_pairs={{0,0},{1,64},{2,128},{3,192},{32,32},{33,96},{34,160},{35,224},{64... | collective-permute-start | bytes 393224 | tf_op jit(solution)/shard_map/ppermute | solution.py:266
  502.4 14.6 %collective-permute-start.9 = (f32[32,1024]{1,0:T(8,128)S(1)}, f32[32,1024]{1,0:T(8,128)S(1)}, u32[]{:S(2)}, u32[]{:S(2)}) collective-permute-start(f32[32,1024]{1,0:T(8,128)S(1)} %get-tuple-element.28), channel_id=1, source_target_pairs={{0,32},{1,96},{2,160},{3,224},{32,0},{33,64},{34,128},{35,192},{64... | collective-permute-start | bytes 393224 | tf_op jit(solution)/shard_map/ppermute | solution.py:266
  503.6 17.2 %collective-permute-start.10 = (f32[32,1024]{1,0:T(8,128)S(1)}, f32[32,1024]{1,0:T(8,128)S(1)}, u32[]{:S(2)}, u32[]{:S(2)}) collective-permute-start(f32[32,1024]{1,0:T(8,128)S(1)} %maximum_select_fusion.3), channel_id=1, source_target_pairs={{0,0},{1,32},{2,64},{3,96},{4,128},{5,160},{6,192},{7,224},{32,1},... | collective-permute-start | bytes 393224 | tf_op jit(solution)/shard_map/ppermute | solution.py:251
